TPU v7x, 256 devices: a whole 4x4x8 slice. The times are simulated.
256 devices in a mesh: band: 128 (over z, y, x), ch: 2 (over core).
Axes of the slice: x: 4, y: 4, z: 8, core: 2. Of those that a mesh axis runs over, the one named last changes fastest.
Arguments:
- grid_field: bfloat16 [100, 2097152], P(None, 'band'), may hold values from -6 to 6
- band_points: int32 [128], P('band'), may hold values from 8192 to 16384
- block_ids: int32 [128, 16], P('band'), may hold values from 0 to 4095, as said below
- block_count: int32 [128], P('band'), may hold values from 8 to 16
- block_weight: bfloat16 [128, 16, 256, 512], P('band'), may hold values from 0 to 0.039794922
- embed_weight: bfloat16 [100, 1024], P(None, 'ch'), may hold values from -0.3125 to 0.3125
- edge_src: int32 [655360], P('band'), may hold values from 0 to 32767, as said below
- edge_dst: int32 [655360], P('band'), may hold values from 0 to 32767, as said below
- edge_in_weight: bfloat16 [2, 1024, 1024], P(None, None, 'ch'), may hold values from -0.1875 to 0.1875
- edge_out_weight: bfloat16 [1024, 1024], P('ch'), may hold values from -0.0625 to 0.0625
- node_in_weight: bfloat16 [2, 1024, 1024], P(None, None, 'ch'), may hold values from -0.125 to 0.125
- node_out_weight: bfloat16 [1024, 1024], P('ch'), may hold values from -0.1875 to 0.1875
Outputs:
- node_state: bfloat16 [32768, 1024], P('band', 'ch')
Inputs may be any that keep to these rules, and one draw needn't show every extreme that they name: For band b, block_ids[b, k] * 512 lies from max(b * 16384 - 16384 // 2, 0) to min((b + 1) * 16384 + 16384 // 2, 2097152) - 512; both ends are named by every band; ids may repeat. `edge_src`: edge e belongs to band b = e // 5120; its source node lies in bands b - 1 to b + 1 of the mesh. `edge_dst`: edge e ends at a node of its band b = e // 5120.
All inputs are finite; a program needn't handle non-finite values.
Results may differ from a plain program's by a relative error of at most 0.015.
Values may be sent and summed in bfloat16 or wider, within the bound.
No kernel may reach another device: no remote copies, remote signals or barrier semaphores. Data moves between devices by JAX's collectives and lax.ppermute only.
A program may use at most 64 MiB of HBM per device.

v0:
```python
import jax
import jax.numpy as jnp
from jax import lax
from jax.experimental import pallas as pl
from jax.experimental.pallas import tpu as pltpu
from jax.sharding import PartitionSpec as P

F32 = jnp.float32
BF16 = jnp.bfloat16
VMEM = pl.BlockSpec(memory_space=pltpu.VMEM)
HBM = pl.BlockSpec(memory_space=pltpu.HBM)
SMEM = pl.BlockSpec(memory_space=pltpu.SMEM)
NT = (((1,), (1,)), ((), ()))
TN = (((0,), (0,)), ((), ()))


def silu(v):
    return v * (0.5 * jnp.tanh(0.5 * v) + 0.5)


def pack_kernel(band_points_ref, points_ref, out_ref, limit_ref, limit_sem, sems):
    core = lax.axis_index("ch")
    half = out_ref.shape[1]
    parts = sems.shape[0]
    width = half // parts
    limit_copy = pltpu.make_async_copy(band_points_ref, limit_ref, limit_sem)
    limit_copy.start()
    copies = []
    for i in range(parts):
        start = pl.multiple_of((1 - core) * half + i * width, width)
        copies.append(
            pltpu.make_async_copy(
                points_ref.at[:, pl.ds(start, width)],
                out_ref.at[:, i * width : (i + 1) * width],
                sems.at[i],
            )
        )
        copies[-1].start()
    limit_copy.wait()
    for i in range(parts):
        copies[i].wait()

        @pl.when((core == 0) & (half + (i + 1) * width > limit_ref[0]))
        def _():
            x = out_ref[:, i * width : (i + 1) * width]
            column = half + i * width + lax.broadcasted_iota(jnp.int32, x.shape, 1)
            out_ref[:, i * width : (i + 1) * width] = jnp.where(
                column < limit_ref[0], x, jnp.zeros_like(x)
            )


def own_kernel(
    ids_ref, count_ref, limit_ref, weight_ref, points_ref, out_ref,
):
    band, core = lax.axis_index("band"), lax.axis_index("ch")
    channels = points_ref.shape[0]
    kblocks, _, block_len = weight_ref.shape
    sub_count = points_ref.shape[1] // block_len
    out_ref[...] = jnp.zeros_like(out_ref)
    for k in range(kblocks):
        local = ids_ref[0, k] - band * sub_count
        mine = (local >= 0) & (local < sub_count) & (core == k % 2) & (k < count_ref[0])

        @pl.when(mine)
        def _():
            at = pl.multiple_of(local * block_len, block_len)
            x = points_ref[:, pl.ds(at, block_len)]
            column = at + lax.broadcasted_iota(jnp.int32, x.shape, 1)
            x = jnp.where(column < limit_ref[0], x, jnp.zeros_like(x))
            out_ref[:channels, :] += lax.dot_general(
                x, weight_ref[k], NT, preferred_element_type=F32
            )


def halo_kernel(ids_ref, count_ref, weight_ref, points_ref, own_ref, out_ref, slots):
    band, core = lax.axis_index("band"), lax.axis_index("ch")
    channels = points_ref.shape[0]
    kblocks, _, block_len = weight_ref.shape
    blocks = points_ref.shape[1] // block_len
    sub_count = 2 * blocks
    found = jnp.int32(0)
    for k in range(kblocks):
        local = ids_ref[0, k] - band * sub_count
        low = (core == 0) & (local < 0)
        high = (core == 1) & (local >= sub_count)
        mine = (low | high) & (k < count_ref[0])
        block = jnp.where(low, local + blocks, local - sub_count)

        @pl.when(mine)
        def _():
            slots[0, found] = k
            slots[1, found] = jnp.clip(block, 0, blocks - 1)

        found = found + mine.astype(jnp.int32)
    out_ref[...] = own_ref[...]
    group = 4
    for first in range(0, kblocks, group):

        @pl.when(first < found)
        def _():
            total = None
            for j in range(first, first + group):
                used = j < found
                k = jnp.where(used, slots[0, j], 0)
                block = jnp.where(used, slots[1, j], 0)
                at = pl.multiple_of(block * block_len, block_len)
                x = points_ref[:, pl.ds(at, block_len)]
                x = jnp.where(used, x, jnp.zeros_like(x))
                part = lax.dot_general(x, weight_ref[k], NT, preferred_element_type=F32)
                total = part if total is None else total + part
            out_ref[:channels, :] += total


def weights_kernel(
    embed_ref, embed_other_ref, edge_in_ref, node_own_ref, node_other_ref,
    out_own_ref, out_other_ref, last_own_hbm, last_other_hbm,
    into_ref, direct_ref, agg_ref, last_ref, sems,
):
    core = lax.axis_index("ch")
    channels, share = embed_ref.shape
    own = pl.ds(pl.multiple_of(core * share, share), share)
    other = pl.ds(pl.multiple_of((1 - core) * share, share), share)

    copies = [
        pltpu.make_async_copy(half.at[:, own], last_ref.at[i], sems.at[i])
        for i, half in enumerate((last_own_hbm, last_other_hbm))
    ]
    for copy in copies:
        copy.start()

    def dot(a, b):
        return jnp.dot(a, b, preferred_element_type=F32)

    rows = direct_ref.shape[0]
    into_ref[...] = jnp.zeros_like(into_ref)
    direct_ref[...] = jnp.zeros_like(direct_ref)
    for i in range(2):
        v = dot(embed_ref[...], edge_in_ref[i, own, :])
        v += dot(embed_other_ref[...], edge_in_ref[i, other, :])
        into_ref[i * rows : i * rows + channels, :] = v.astype(BF16)
    for j, node_ref in enumerate((node_own_ref, node_other_ref)):
        columns = slice(j * share, (j + 1) * share)
        v = dot(embed_ref[...], node_ref[0, own, :])
        v += dot(embed_other_ref[...], node_ref[0, other, :])
        direct_ref[:channels, columns] = v.astype(BF16)
        for i, half_ref in enumerate((out_own_ref, out_other_ref)):
            agg_ref[i, :, columns] = dot(half_ref[...], node_ref[1]).astype(BF16)
    for copy in copies:
        copy.wait()


def edge_kernel(near_ref, other_ref, mid_ref, into_ref, src_ref, dst_ref, out_ref, acc_ref):
    band = lax.axis_index("band")
    rows, nodes = mid_ref.shape
    edges = src_ref.shape[1]
    size = edges // 2
    first = lax.axis_index("ch") == 0
    low = jnp.where(first, near_ref[...], other_ref[...])
    high = jnp.where(first, other_ref[...], near_ref[...])
    sources = jnp.concatenate([low, mid_ref[...], high], axis=0)
    node = lax.broadcasted_iota(jnp.int32, (nodes, size), 0).astype(F32).astype(BF16)
    one, zero = jnp.ones((), BF16), jnp.zeros((), BF16)

    def before(at):
        src = src_ref[:, at : at + size] - (band - 1) * nodes
        dst = dst_ref[:, at : at + size] - band * nodes
        piece = src // nodes
        from_hot = jnp.where(node == (src - piece * nodes).astype(F32).astype(BF16), one, zero)
        to_hot = jnp.where(node == dst.astype(F32).astype(BF16), one, zero)
        got = jnp.dot(sources, from_hot, preferred_element_type=F32)
        a, b, c = got[:rows], got[rows : 2 * rows], got[2 * rows :]
        from_src = jnp.where(piece == 0, a, jnp.where(piece == 1, b, c))
        from_dst = jnp.dot(mid_ref[...], to_hot, preferred_element_type=F32)
        both = jnp.concatenate([from_src.astype(BF16), from_dst.astype(BF16)], axis=0)
        return lax.dot_general(into_ref[...], both, TN, preferred_element_type=F32), to_hot

    acc_ref[...] = jnp.zeros_like(acc_ref)
    now = before(0)
    for at in range(0, edges, size):
        later = before(at + size) if at + size < edges else None
        pre, to_hot = now
        hidden = silu(pre).astype(BF16)
        acc_ref[...] += lax.dot_general(to_hot, hidden, NT, preferred_element_type=F32)
        now = later
    out_ref[...] = acc_ref[...].astype(out_ref.dtype)


def node_kernel(own_ref, other_ref, mid_ref, direct_ref, embed_ref, agg_ref, last_ref, out_ref):
    channels, share = embed_ref.shape
    v = lax.dot_general(mid_ref[...], direct_ref[...], TN, preferred_element_type=F32)
    v += jnp.dot(own_ref[...], agg_ref[0], preferred_element_type=F32)
    v += jnp.dot(other_ref[...], agg_ref[1], preferred_element_type=F32)
    update = silu(v).astype(BF16)
    v = lax.dot_general(mid_ref[:channels, :], embed_ref[...], TN, preferred_element_type=F32)
    v += jnp.dot(update[:, :share], last_ref[0], preferred_element_type=F32)
    v += jnp.dot(update[:, share:], last_ref[1], preferred_element_type=F32)
    out_ref[...] = v.astype(out_ref.dtype)


def call(kernel, out, specs, limit_mib, flops, args, scratch=()):
    return pl.pallas_call(
        kernel,
        out_shape=out,
        in_specs=specs,
        out_specs=[VMEM] * len(out) if isinstance(out, tuple) else VMEM,
        scratch_shapes=list(scratch),
        compiler_params=pltpu.CompilerParams(vmem_limit_bytes=int(limit_mib * 2**20)),
        cost_estimate=pl.CostEstimate(flops=flops, bytes_accessed=1 << 20, transcendentals=0),
    )(*args)


def on_device(
    grid_field,
    band_points,
    block_ids,
    block_count,
    block_weight,
    embed_weight,
    edge_src,
    edge_dst,
    edge_in_weight,
    edge_out_weight,
    node_in_weight,
    node_out_weight,
):
    bands = lax.axis_size("band")
    channels, points = grid_field.shape
    _, kblocks, nodes, block_len = block_weight.shape
    share = embed_weight.shape[1]
    edges = edge_src.shape[0]
    half = points // 2
    rows = -(-channels // 16) * 16
    weight = block_weight[0]
    shape = jax.ShapeDtypeStruct

    pairs = [(2 * b, 2 * b + 2) for b in range(bands - 1)] + [(2 * bands - 2, 2 * bands - 1)]
    pairs += [(2 * b + 3, 2 * b + 1) for b in range(bands - 1)] + [(1, 0)]
    piece = call(
        pack_kernel,
        pltpu.VMEM((channels, half), BF16),
        [HBM, HBM],
        61,
        1 << 20,
        (band_points, grid_field),
        [pltpu.SMEM((1,), jnp.int32), pltpu.SemaphoreType.DMA, pltpu.SemaphoreType.DMA((8,))],
    )
    halo = lax.ppermute(piece, ("band", "ch"), pairs)

    def partner(x):
        return lax.ppermute(x, "ch", [(0, 1), (1, 0)])

    embed_other = partner(embed_weight)
    out_other = partner(edge_out_weight)
    node_other = partner(node_in_weight)
    last_other = partner(node_out_weight)
    src, dst = edge_src.reshape(1, edges), edge_dst.reshape(1, edges)
    remap_flops = 2 * channels * nodes * block_len * kblocks // 4
    sums = shape((rows, nodes), F32)
    partial = call(
        own_kernel,
        sums,
        [SMEM] * 3 + [VMEM] * 2,
        16,
        8 * remap_flops,
        (block_ids, block_count, band_points, weight, grid_field),
    )
    into_edge, direct, agg, last = call(
        weights_kernel,
        (
            shape((2 * rows, share), BF16),
            shape((rows, 2 * share), BF16),
            shape((2, share, 2 * share), BF16),
            shape((2, share, share), BF16),
        ),
        [VMEM] * 7 + [HBM] * 2,
        18,
        16 * share**3,
        (
            embed_weight,
            embed_other,
            edge_in_weight,
            node_in_weight,
            node_other,
            edge_out_weight,
            out_other,
            node_out_weight,
            last_other,
        ),
        [pltpu.SemaphoreType.DMA((2,))],
    )

    partial = call(
        halo_kernel,
        sums,
        [SMEM] * 2 + [VMEM] * 3,
        12,
        remap_flops,
        (block_ids, block_count, weight, halo, partial),
        [pltpu.SMEM((2, kblocks), jnp.int32)],
    )
    mid = (partial + partner(partial)).astype(BF16)
    near = lax.ppermute(mid, ("band", "ch"), pairs)
    near_other = partner(near)
    by_node = call(
        edge_kernel,
        shape((nodes, share), BF16),
        [VMEM] * 6,
        24,
        2 * edges * nodes * 7 * 256,
        (near, near_other, mid, into_edge, src, dst),
        [pltpu.VMEM((nodes, share), F32)],
    )
    return call(
        node_kernel,
        shape((nodes, share), BF16),
        [VMEM] * 7,
        12,
        2 * nodes * share * 6 * share,
        (by_node, partner(by_node), mid, direct, embed_weight, agg, last),
    )


def solution(mesh):
    return jax.shard_map(
        on_device,
        mesh=mesh,
        in_specs=(
            P(None, "band"),
            P("band"),
            P("band", None),
            P("band"),
            P("band", None, None, None),
            P(None, "ch"),
            P("band"),
            P("band"),
            P(None, None, "ch"),
            P("ch", None),
            P(None, None, "ch"),
            P("ch", None),
        ),
        out_specs=P("band", "ch"),
        check_vma=False,
    )
```

profile of v0, /device:TPU:129, one launch (start us, length us, event | category | flops | bytes accessed | tf_op | source)
XLA Modules:
  0.0 55.6 jit_solution(1447767923763739369)
XLA Ops:
  0.0 0.7 %collective-permute-start.5 = (bf16[2,1024,512]{2,1,0:T(8,128)(2,1)}, bf16[2,1024,512]{2,1,0:T(8,128)(2,1)}, u32[]{:S(2)}, u32[]{:S(2)}) collective-permute-start(bf16[2,1024,512]{2,1,0:T(8,128)(2,1)} %node_own_ref.1), channel_id=1, source_target_pairs={{0,1},{1,0},{2,3},{3,2},{4,5},{5,4},{6,7},{7,6},{8,9},{9,8},{10,11... | collective-permute-start | bytes 6291464 | tf_op jit(solution)/shard_map/ppermute | solution.py:250
  1.3 1.7 %shard_map.118 = bf16[100,8192]{1,0:T(8,128)(2,1)S(1)} custom-call(s32[1]{0:T(128)S(6)} %copy.13.band_points_ref.limit_ref, bf16[100,16384]{1,0:T(8,128)(2,1)} %points_ref.3), custom_call_target="tpu_custom_call" | custom-call | flops 1048576 | bytes 1048576 | tf_op jit(solution)/shard_map/pallas_call | solution.py:201
  3.0 4.5 %collective-permute-start = (bf16[100,8192]{1,0:T(8,128)(2,1)S(1)}, bf16[100,8192]{1,0:T(8,128)(2,1)S(1)}, u32[]{:S(2)}, u32[]{:S(2)}) collective-permute-start(bf16[100,8192]{1,0:T(8,128)(2,1)S(1)} %shard_map.118), channel_id=1, source_target_pairs={{0,2},{2,4},{4,6},{6,8},{8,10},{10,12},{12,14},{14,16},{16,18},{18... | collective-permute-start | bytes 4915208 | tf_op jit(solution)/shard_map/ppermute | solution.py:247
  7.6 0.5 collective-permute-start.7
  8.8 0.0 copy-start
  8.8 2.2 %copy-done = bf16[1,16,256,512]{3,2,1,0:T(8,128)(2,1)S(1)} copy-done((bf16[1,16,256,512]{3,2,1,0:T(8,128)(2,1)S(1)}, bf16[1,16,256,512]{3,2,1,0:T(8,128)(2,1)}, u32[]{:S(2)}) %copy-start) | copy-done | bytes 4194328
  10.9 2.0 %copy-done.1 = bf16[100,16384]{1,0:T(8,128)(2,1)S(1)} copy-done((bf16[100,16384]{1,0:T(8,128)(2,1)S(1)}, bf16[100,16384]{1,0:T(8,128)(2,1)}, u32[]{:S(2)}) %copy-start.1) | copy-done | bytes 3276824
  12.9 0.9 %shard_map.119.own_ref = f32[112,256]{1,0:T(8,128)S(1)} custom-call(s32[1,16]{1,0:T(1,128)S(1)} %copy-done.7, s32[1]{0:T(128)S(6)} %copy.14.count_ref, s32[1]{0:T(128)S(6)} %copy.13.band_points_ref.limit_ref, bf16[16,256,512]{2,1,0:T(8,128)(2,1)S(1)} %bitcast.3, bf16[100,16384]{1,0:T(8,128)(2,1)S(1)} %copy-done.1), custom_call_target="tpu_custom_call" | custom-call | flops 838860800 | bytes 1048576 | tf_op jit(solution)/shard_map/pallas_call | solution.py:201
  13.8 0.0 copy-start.6
  13.9 0.0 copy-start.2
  13.9 0.0 copy-start.5
  13.9 12.4 %collective-permute-done.points_ref = bf16[100,8192]{1,0:T(8,128)(2,1)S(1)} collective-permute-done((bf16[100,8192]{1,0:T(8,128)(2,1)S(1)}, bf16[100,8192]{1,0:T(8,128)(2,1)S(1)}, u32[]{:S(2)}, u32[]{:S(2)}) %collective-permute-start) | collective-permute-done | bytes 1638432 | tf_op jit(solution)/shard_map/ppermute | solution.py:247
  26.3 1.2 %shard_map.120 = f32[112,256]{1,0:T(8,128)S(1)} custom-call(s32[1,16]{1,0:T(1,128)S(1)} %copy-done.7, s32[1]{0:T(128)S(6)} %copy.14.count_ref, bf16[16,256,512]{2,1,0:T(8,128)(2,1)S(1)} %bitcast.4, bf16[100,8192]{1,0:T(8,128)(2,1)S(1)} %collective-permute-done.points_ref, f32[112,256]{1,0:T(8,128)S(1)} %shard_map.119.own_ref), custom_call_target="tpu_custom_call" | custom-call | flops 104857600 | bytes 1048576 | tf_op jit(solution)/shard_map/pallas_call | solution.py:201
  27.5 4.1 %collective-permute-start.1 = (f32[112,256]{1,0:T(8,128)S(1)}, f32[112,256]{1,0:T(8,128)S(1)}, u32[]{:S(2)}, u32[]{:S(2)}) collective-permute-start(f32[112,256]{1,0:T(8,128)S(1)} %shard_map.120), channel_id=1, source_target_pairs={{0,1},{1,0},{2,3},{3,2},{4,5},{5,4},{6,7},{7,6},{8,9},{9,8},{10,11... | collective-permute-start | bytes 344072 | tf_op jit(solution)/shard_map/ppermute | solution.py:250
  31.6 0.1 collective-permute-start.4
  31.7 0.9 %collective-permute-done.1 = f32[112,256]{1,0:T(8,128)S(1)} collective-permute-done((f32[112,256]{1,0:T(8,128)S(1)}, f32[112,256]{1,0:T(8,128)S(1)}, u32[]{:S(2)}, u32[]{:S(2)}) %collective-permute-start.1) | collective-permute-done | bytes 114720 | tf_op jit(solution)/shard_map/ppermute | solution.py:250
  32.6 4.2 %collective-permute-start.2 = (bf16[112,256]{1,0:T(8,128)(2,1)S(1)}, bf16[112,256]{1,0:T(8,128)(2,1)S(1)}, u32[]{:S(2)}, u32[]{:S(2)}) collective-permute-start(bf16[112,256]{1,0:T(8,128)(2,1)S(1)} %add_convert_fusion.mid_ref), channel_id=1, source_target_pairs={{0,2},{2,4},{4,6},{6,8},{8,10},{10,12},{12,14},{14,16},{16,18},{18... | collective-permute-start | bytes 172040 | tf_op jit(solution)/shard_map/ppermute | solution.py:302
  36.8 1.3 %collective-permute-done.2.near_ref = bf16[112,256]{1,0:T(8,128)(2,1)S(1)} collective-permute-done((bf16[112,256]{1,0:T(8,128)(2,1)S(1)}, bf16[112,256]{1,0:T(8,128)(2,1)S(1)}, u32[]{:S(2)}, u32[]{:S(2)}) %collective-permute-start.2) | collective-permute-done | bytes 57376 | tf_op jit(solution)/shard_map/ppermute | solution.py:302
  38.1 4.6 %collective-permute-start.3 = (bf16[112,256]{1,0:T(8,128)(2,1)S(1)}, bf16[112,256]{1,0:T(8,128)(2,1)S(1)}, u32[]{:S(2)}, u32[]{:S(2)}) collective-permute-start(bf16[112,256]{1,0:T(8,128)(2,1)S(1)} %collective-permute-done.2.near_ref), channel_id=1, source_target_pairs={{0,1},{1,0},{2,3},{3,2},{4,5},{5,4},{6,7},{7,6},{8,9},{9,8},{10,11... | collective-permute-start | bytes 172040 | tf_op jit(solution)/shard_map/ppermute | solution.py:250
  42.7 4.7 %shard_map.121 = (bf16[224,512]{1,0:T(8,128)(2,1)S(1)}, bf16[112,1024]{1,0:T(8,128)(2,1)S(1)}, bf16[2,512,1024]{2,1,0:T(8,128)(2,1)S(1)}, bf16[2,512,512]{2,1,0:T(8,128)(2,1)S(1)}) custom-call(bf16[100,512]{1,0:T(8,128)(2,1)S(1)} %copy-done.6, bf16[100,512]{1,0:T(8,128)(2,1)S(1)} %collective-permute-done.4.embed_other_ref, ...), custom_call_target="tpu_custom_call" | custom-call | flops 2147483648 | bytes 1048576 | tf_op jit(solution)/shard_map/pallas_call | solution.py:201
  47.5 4.6 %shard_map.122.own_ref = bf16[256,512]{1,0:T(8,128)(2,1)S(1)} custom-call(bf16[112,256]{1,0:T(8,128)(2,1)S(1)} %collective-permute-done.2.near_ref, bf16[112,256]{1,0:T(8,128)(2,1)S(1)} %collective-permute-done.3.other_ref, bf16[112,256]{1,0:T(8,128)(2,1)S(1)} %add_convert_fusion.mid_ref, bf16[224,512]{1,0:T(8,128)(2,1)S(1)} %get-tuple-element.9.into_ref, ...), custom_call_target="tpu_custom_call" | custom-call | flops 4697620480 | bytes 1048576 | tf_op jit(solution)/shard_map/pallas_call | solution.py:201
  52.1 0.1 collective-permute-start.8
  52.2 1.5 %collective-permute-done.8.other_ref = bf16[256,512]{1,0:T(8,128)(2,1)S(1)} collective-permute-done((bf16[256,512]{1,0:T(8,128)(2,1)S(1)}, bf16[256,512]{1,0:T(8,128)(2,1)S(1)}, u32[]{:S(2)}, u32[]{:S(2)}) %collective-permute-start.8) | collective-permute-done | bytes 262176 | tf_op jit(solution)/shard_map/ppermute | solution.py:250
  53.7 1.9 %shard_map.123 = bf16[256,512]{1,0:T(8,128)(2,1)} custom-call(bf16[256,512]{1,0:T(8,128)(2,1)S(1)} %shard_map.122.own_ref, bf16[256,512]{1,0:T(8,128)(2,1)S(1)} %collective-permute-done.8.other_ref, bf16[112,256]{1,0:T(8,128)(2,1)S(1)} %add_convert_fusion.mid_ref, bf16[112,1024]{1,0:T(8,128)(2,1)S(1)} %get-tuple-element.10.direct_ref, ...), custom_call_target="tpu_custom_call" | custom-call | flops 805306368 | bytes 1048576 | tf_op jit(solution)/shard_map/pallas_call | solution.py:201
  (21 shorter events, 0.1 us)
Async XLA Ops:
  0.0 42.7 %collective-permute-start.5 = (bf16[2,1024,512]{2,1,0:T(8,128)(2,1)}, bf16[2,1024,512]{2,1,0:T(8,128)(2,1)}, u32[]{:S(2)}, u32[]{:S(2)}) collective-permute-start(bf16[2,1024,512]{2,1,0:T(8,128)(2,1)} %node_own_ref.1), channel_id=1, source_target_pairs={{0,1},{1,0},{2,3},{3,2},{4,5},{5,4},{6,7},{7,6},{8,9},{9,8},{10,11... | collective-permute-start | bytes 6291464 | tf_op jit(solution)/shard_map/ppermute | solution.py:250
  1.3 6.3 %copy-start.4 = (bf16[512,1024]{1,0:T(8,128)(2,1)S(1)}, bf16[512,1024]{1,0:T(8,128)(2,1)}, u32[]{:S(2)}) copy-start(bf16[512,1024]{1,0:T(8,128)(2,1)} %out_own_ref.1) | copy-start | bytes 3145732
  1.3 7.4 %copy-start.7 = (s32[1,16]{1,0:T(1,128)S(1)}, s32[1,16]{1,0:T(1,128)}, u32[]{:S(2)}) copy-start(s32[1,16]{1,0:T(1,128)} %ids_ref.3) | copy-start | bytes 196
  3.0 23.3 %collective-permute-start = (bf16[100,8192]{1,0:T(8,128)(2,1)S(1)}, bf16[100,8192]{1,0:T(8,128)(2,1)S(1)}, u32[]{:S(2)}, u32[]{:S(2)}) collective-permute-start(bf16[100,8192]{1,0:T(8,128)(2,1)S(1)} %shard_map.118), channel_id=1, source_target_pairs={{0,2},{2,4},{4,6},{6,8},{8,10},{10,12},{12,14},{14,16},{16,18},{18... | collective-permute-start | bytes 4915208 | tf_op jit(solution)/shard_map/ppermute | solution.py:247
  7.6 35.1 %collective-permute-start.6 = (bf16[512,1024]{1,0:T(8,128)(2,1)S(1)}, bf16[512,1024]{1,0:T(8,128)(2,1)S(1)}, u32[]{:S(2)}, u32[]{:S(2)}) collective-permute-start(bf16[512,1024]{1,0:T(8,128)(2,1)S(1)} %copy-done.4), channel_id=1, source_target_pairs={{0,1},{1,0},{2,3},{3,2},{4,5},{5,4},{6,7},{7,6},{8,9},{9,8},{10,11... | collective-permute-start | bytes 3145736 | tf_op jit(solution)/shard_map/ppermute | solution.py:250
  7.6 35.1 %collective-permute-start.7 = (bf16[512,1024]{1,0:T(8,128)(2,1)}, bf16[512,1024]{1,0:T(8,128)(2,1)S(1)}, u32[]{:S(2)}, u32[]{:S(2)}) collective-permute-start(bf16[512,1024]{1,0:T(8,128)(2,1)} %last_own_hbm.1), channel_id=1, source_target_pairs={{0,1},{1,0},{2,3},{3,2},{4,5},{5,4},{6,7},{7,6},{8,9},{9,8},{10,11... | collective-permute-start | bytes 3145736 | tf_op jit(solution)/shard_map/ppermute | solution.py:250
  8.8 2.2 %copy-start = (bf16[1,16,256,512]{3,2,1,0:T(8,128)(2,1)S(1)}, bf16[1,16,256,512]{3,2,1,0:T(8,128)(2,1)}, u32[]{:S(2)}) copy-start(bf16[1,16,256,512]{3,2,1,0:T(8,128)(2,1)} %param.16) | copy-start | bytes 12582916
  10.9 2.0 %copy-start.1 = (bf16[100,16384]{1,0:T(8,128)(2,1)S(1)}, bf16[100,16384]{1,0:T(8,128)(2,1)}, u32[]{:S(2)}) copy-start(bf16[100,16384]{1,0:T(8,128)(2,1)} %points_ref.3) | copy-start | bytes 9830404
  13.8 17.8 %copy-start.6 = (bf16[100,512]{1,0:T(8,128)(2,1)S(1)}, bf16[100,512]{1,0:T(8,128)(2,1)}, u32[]{:S(2)}) copy-start(bf16[100,512]{1,0:T(8,128)(2,1)} %embed_ref.3) | copy-start | bytes 307204
  13.9 28.9 %copy-start.2 = (bf16[2,1024,512]{2,1,0:T(8,128)(2,1)S(1)}, bf16[2,1024,512]{2,1,0:T(8,128)(2,1)}, u32[]{:S(2)}) copy-start(bf16[2,1024,512]{2,1,0:T(8,128)(2,1)} %edge_in_ref.1) | copy-start | bytes 6291460
  13.9 28.9 %copy-start.3 = (bf16[2,1024,512]{2,1,0:T(8,128)(2,1)S(1)}, bf16[2,1024,512]{2,1,0:T(8,128)(2,1)}, u32[]{:S(2)}) copy-start(bf16[2,1024,512]{2,1,0:T(8,128)(2,1)} %node_own_ref.1) | copy-start | bytes 6291460
  13.9 28.8 %copy-start.5 = (bf16[512,1024]{1,0:T(8,128)(2,1)S(1)}, bf16[512,1024]{1,0:T(8,128)(2,1)}, u32[]{:S(2)}) copy-start(bf16[512,1024]{1,0:T(8,128)(2,1)} %last_own_hbm.1) | copy-start | bytes 3145732
  27.5 5.1 %collective-permute-start.1 = (f32[112,256]{1,0:T(8,128)S(1)}, f32[112,256]{1,0:T(8,128)S(1)}, u32[]{:S(2)}, u32[]{:S(2)}) collective-permute-start(f32[112,256]{1,0:T(8,128)S(1)} %shard_map.120), channel_id=1, source_target_pairs={{0,1},{1,0},{2,3},{3,2},{4,5},{5,4},{6,7},{7,6},{8,9},{9,8},{10,11... | collective-permute-start | bytes 344072 | tf_op jit(solution)/shard_map/ppermute | solution.py:250
  31.6 11.1 %collective-permute-start.4 = (bf16[100,512]{1,0:T(8,128)(2,1)S(1)}, bf16[100,512]{1,0:T(8,128)(2,1)S(1)}, u32[]{:S(2)}, u32[]{:S(2)}) collective-permute-start(bf16[100,512]{1,0:T(8,128)(2,1)S(1)} %copy-done.6), channel_id=1, source_target_pairs={{0,1},{1,0},{2,3},{3,2},{4,5},{5,4},{6,7},{7,6},{8,9},{9,8},{10,11... | collective-permute-start | bytes 307208 | tf_op jit(solution)/shard_map/ppermute | solution.py:250
  32.6 14.8 %copy-start.8 = (s32[5120]{0:T(1024)S(1)}, s32[5120]{0:T(1024)}, u32[]{:S(2)}) copy-start(s32[5120]{0:T(1024)} %param.18) | copy-start | bytes 61444
  32.6 14.8 %copy-start.9 = (s32[5120]{0:T(1024)S(1)}, s32[5120]{0:T(1024)}, u32[]{:S(2)}) copy-start(s32[5120]{0:T(1024)} %param.19) | copy-start | bytes 61444
  32.6 5.4 %collective-permute-start.2 = (bf16[112,256]{1,0:T(8,128)(2,1)S(1)}, bf16[112,256]{1,0:T(8,128)(2,1)S(1)}, u32[]{:S(2)}, u32[]{:S(2)}) collective-permute-start(bf16[112,256]{1,0:T(8,128)(2,1)S(1)} %add_convert_fusion.mid_ref), channel_id=1, source_target_pairs={{0,2},{2,4},{4,6},{6,8},{8,10},{10,12},{12,14},{14,16},{16,18},{18... | collective-permute-start | bytes 172040 | tf_op jit(solution)/shard_map/ppermute | solution.py:302
  38.1 9.3 %collective-permute-start.3 = (bf16[112,256]{1,0:T(8,128)(2,1)S(1)}, bf16[112,256]{1,0:T(8,128)(2,1)S(1)}, u32[]{:S(2)}, u32[]{:S(2)}) collective-permute-start(bf16[112,256]{1,0:T(8,128)(2,1)S(1)} %collective-permute-done.2.near_ref), channel_id=1, source_target_pairs={{0,1},{1,0},{2,3},{3,2},{4,5},{5,4},{6,7},{7,6},{8,9},{9,8},{10,11... | collective-permute-start | bytes 172040 | tf_op jit(solution)/shard_map/ppermute | solution.py:250
  52.1 1.6 %collective-permute-start.8 = (bf16[256,512]{1,0:T(8,128)(2,1)S(1)}, bf16[256,512]{1,0:T(8,128)(2,1)S(1)}, u32[]{:S(2)}, u32[]{:S(2)}) collective-permute-start(bf16[256,512]{1,0:T(8,128)(2,1)S(1)} %shard_map.122.own_ref), channel_id=1, source_target_pairs={{0,1},{1,0},{2,3},{3,2},{4,5},{5,4},{6,7},{7,6},{8,9},{9,8},{10,11... | collective-permute-start | bytes 786440 | tf_op jit(solution)/shard_map/ppermute | solution.py:250
where the time goes:
time: 55.8 us; the launch traced here: 55.6 us
  starting transfers between devices  18.9 us (34%)
  waiting for transfers between devices  16.1 us (29%)
  Pallas kernels  14.9 us (27%)
  local copies, waits for them, and re-layouts  4.19 us (8%)
  between operations  1.49 us (3%)
    pallas_call x6, Pallas kernels, call(): pl.pallas_call(kernel, out_shape=out, in_specs=specs, out_specs=[VMEM] *...  14.9 us
    ppermute x1, waiting for transfers between devices, on_device(): halo = lax.ppermute(piece, ('band', 'ch'), pairs)  12.4 us
    ppermute x7, starting transfers between devices, partner(): return lax.ppermute(x, 'ch', [(0, 1), (1, 0)])  10.1 us
    ppermute x1, starting transfers between devices, on_device(): halo = lax.ppermute(piece, ('band', 'ch'), pairs)  4.55 us
    ppermute x1, starting transfers between devices, on_device(): near = lax.ppermute(mid, ('band', 'ch'), pairs)  4.19 us
    unnamed x20, local copies, waits for them, and re-layouts  4.19 us
    ppermute x7, waiting for transfers between devices, partner(): return lax.ppermute(x, 'ch', [(0, 1), (1, 0)])  2.39 us
    ppermute x1, waiting for transfers between devices, on_device(): near = lax.ppermute(mid, ('band', 'ch'), pairs)  1.26 us
  transfers between devices with their start and end apart: 9, of which 4 were waited for; matrix products, arithmetic and copies ran while one was open for 0% of the time, Pallas kernels for 15%

commit v1 on v0

--- a/solution.py
+++ b/solution.py
@@ -1,3 +1,5 @@
+import functools
+
 import jax
 import jax.numpy as jnp
 from jax import lax
@@ -18,9 +20,9 @@
     return v * (0.5 * jnp.tanh(0.5 * v) + 0.5)
 
 
-def pack_kernel(band_points_ref, points_ref, out_ref, limit_ref, limit_sem, sems):
+def pack_kernel(band_points_ref, points_ref, out_ref, rows_ref, limit_ref, limit_sem, sems):
     core = lax.axis_index("ch")
-    half = out_ref.shape[1]
+    channels, half = rows_ref.shape
     parts = sems.shape[0]
     width = half // parts
     limit_copy = pltpu.make_async_copy(band_points_ref, limit_ref, limit_sem)
@@ -31,22 +33,27 @@
         copies.append(
             pltpu.make_async_copy(
                 points_ref.at[:, pl.ds(start, width)],
-                out_ref.at[:, i * width : (i + 1) * width],
+                rows_ref.at[:, i * width : (i + 1) * width],
                 sems.at[i],
             )
         )
         copies[-1].start()
     limit_copy.wait()
+    limit = jnp.where(core == 0, limit_ref[0] - half, half)
+    full = channels // 8
+    last = channels - 8 * full
     for i in range(parts):
         copies[i].wait()
-
-        @pl.when((core == 0) & (half + (i + 1) * width > limit_ref[0]))
-        def _():
-            x = out_ref[:, i * width : (i + 1) * width]
-            column = half + i * width + lax.broadcasted_iota(jnp.int32, x.shape, 1)
-            out_ref[:, i * width : (i + 1) * width] = jnp.where(
-                column < limit_ref[0], x, jnp.zeros_like(x)
-            )
+        at = i * width
+        live = at + lax.broadcasted_iota(jnp.int32, (8, width), 1) < limit
+        for t in range(full):
+            x = rows_ref[8 * t : 8 * t + 8, at : at + width]
+            out_ref[:, t * half + at : t * half + at + width] = jnp.where(live, x, jnp.zeros_like(x))
+        x = rows_ref[8 * full :, at : at + width]
+        x = jnp.where(live[:last], x, jnp.zeros_like(x))
+        low = at % (half * last // 8)
+        row = (at // (half * last // 8)) * last
+        out_ref[row : row + last, full * half + low : full * half + low + width] = x
 
 
 def own_kernel(
@@ -72,12 +79,41 @@
             )
 
 
-def halo_kernel(ids_ref, count_ref, weight_ref, points_ref, own_ref, out_ref, slots):
+def hots_kernel(src_ref, dst_ref, from_ref, to_ref):
+    band = lax.axis_index("band")
+    nodes, edges = from_ref.shape
+    size = edges // 10
+    node = lax.broadcasted_iota(jnp.int32, (nodes, size), 0).astype(F32).astype(BF16)
+    one, zero = jnp.ones((), BF16), jnp.zeros((), BF16)
+    for at in range(0, edges, size):
+        src = src_ref[:, at : at + size] - (band - 1) * nodes
+        src = src - (src // nodes) * nodes
+        dst = dst_ref[:, at : at + size] - band * nodes
+        from_ref[:, at : at + size] = jnp.where(node == src.astype(F32).astype(BF16), one, zero)
+        to_ref[:, at : at + size] = jnp.where(node == dst.astype(F32).astype(BF16), one, zero)
+
+
+def gather_kernel(mid_ref, src_ref, from_ref, to_ref, out_ref):
+    band = lax.axis_index("band")
+    rows, nodes = mid_ref.shape
+    edges = src_ref.shape[1]
+    size = edges // 2
+    for at in range(0, edges, size):
+        piece = (src_ref[:, at : at + size] - (band - 1) * nodes) // nodes
+        got = jnp.dot(mid_ref[...], from_ref[:, at : at + size], preferred_element_type=F32)
+        out_ref[:rows, at : at + size] = jnp.where(piece == 1, got, 0.0).astype(BF16)
+        got = jnp.dot(mid_ref[...], to_ref[:, at : at + size], preferred_element_type=F32)
+        out_ref[rows:, at : at + size] = got.astype(BF16)
+
+
+def halo_kernel(channels, ids_ref, count_ref, weight_ref, points_ref, own_ref, out_ref, slots):
     band, core = lax.axis_index("band"), lax.axis_index("ch")
-    channels = points_ref.shape[0]
     kblocks, _, block_len = weight_ref.shape
-    blocks = points_ref.shape[1] // block_len
+    half = points_ref.shape[1] * 8 // channels
+    blocks = half // block_len
     sub_count = 2 * blocks
+    full = channels // 8
+    last = channels - 8 * full
     found = jnp.int32(0)
     for k in range(kblocks):
         local = ids_ref[0, k] - band * sub_count
@@ -104,8 +140,16 @@
                 k = jnp.where(used, slots[0, j], 0)
                 block = jnp.where(used, slots[1, j], 0)
                 at = pl.multiple_of(block * block_len, block_len)
-                x = points_ref[:, pl.ds(at, block_len)]
-                x = jnp.where(used, x, jnp.zeros_like(x))
+                x = [
+                    points_ref[:, pl.ds(pl.multiple_of(t * half + at, block_len), block_len)]
+                    for t in range(full)
+                ]
+                stack = half * last // 8
+                low = pl.multiple_of(full * half + lax.rem(at, stack), block_len)
+                tail = points_ref[:, pl.ds(low, block_len)].astype(F32)
+                tail = jnp.where(at < stack, tail[:last], tail[last : 2 * last])
+                x = jnp.concatenate([piece.astype(F32) for piece in x] + [tail], axis=0)
+                x = jnp.where(used, x, 0.0).astype(BF16)
                 part = lax.dot_general(x, weight_ref[k], NT, preferred_element_type=F32)
                 total = part if total is None else total + part
             out_ref[:channels, :] += total
@@ -149,38 +193,34 @@
         copy.wait()
 
 
-def edge_kernel(near_ref, other_ref, mid_ref, into_ref, src_ref, dst_ref, out_ref, acc_ref):
+def edge_kernel(
+    near_ref, far_ref, into_ref, src_ref, from_ref, to_ref, gathered_ref, out_ref, acc_ref
+):
     band = lax.axis_index("band")
-    rows, nodes = mid_ref.shape
+    rows, nodes = near_ref.shape
     edges = src_ref.shape[1]
     size = edges // 2
-    first = lax.axis_index("ch") == 0
-    low = jnp.where(first, near_ref[...], other_ref[...])
-    high = jnp.where(first, other_ref[...], near_ref[...])
-    sources = jnp.concatenate([low, mid_ref[...], high], axis=0)
-    node = lax.broadcasted_iota(jnp.int32, (nodes, size), 0).astype(F32).astype(BF16)
-    one, zero = jnp.ones((), BF16), jnp.zeros((), BF16)
+    even = lax.rem(band, 2) == 0
+    low = jnp.where(even, far_ref[...], near_ref[...])
+    high = jnp.where(even, near_ref[...], far_ref[...])
+    sources = jnp.concatenate([low, high], axis=0)
 
     def before(at):
-        src = src_ref[:, at : at + size] - (band - 1) * nodes
-        dst = dst_ref[:, at : at + size] - band * nodes
-        piece = src // nodes
-        from_hot = jnp.where(node == (src - piece * nodes).astype(F32).astype(BF16), one, zero)
-        to_hot = jnp.where(node == dst.astype(F32).astype(BF16), one, zero)
-        got = jnp.dot(sources, from_hot, preferred_element_type=F32)
-        a, b, c = got[:rows], got[rows : 2 * rows], got[2 * rows :]
-        from_src = jnp.where(piece == 0, a, jnp.where(piece == 1, b, c))
-        from_dst = jnp.dot(mid_ref[...], to_hot, preferred_element_type=F32)
-        both = jnp.concatenate([from_src.astype(BF16), from_dst.astype(BF16)], axis=0)
-        return lax.dot_general(into_ref[...], both, TN, preferred_element_type=F32), to_hot
+        piece = (src_ref[:, at : at + size] - (band - 1) * nodes) // nodes
+        got = jnp.dot(sources, from_ref[:, at : at + size], preferred_element_type=F32)
+        got = jnp.where(piece == 0, got[:rows], jnp.where(piece == 2, got[rows:], 0.0))
+        from_src = got.astype(BF16) + gathered_ref[:rows, at : at + size]
+        both = jnp.concatenate([from_src, gathered_ref[rows:, at : at + size]], axis=0)
+        return lax.dot_general(into_ref[...], both, TN, preferred_element_type=F32)
 
     acc_ref[...] = jnp.zeros_like(acc_ref)
     now = before(0)
     for at in range(0, edges, size):
         later = before(at + size) if at + size < edges else None
-        pre, to_hot = now
-        hidden = silu(pre).astype(BF16)
-        acc_ref[...] += lax.dot_general(to_hot, hidden, NT, preferred_element_type=F32)
+        hidden = silu(now.astype(BF16))
+        acc_ref[...] += lax.dot_general(
+            to_ref[:, at : at + size], hidden, NT, preferred_element_type=F32
+        )
         now = later
     out_ref[...] = acc_ref[...].astype(out_ref.dtype)
 
@@ -237,12 +277,17 @@
     pairs += [(2 * b + 3, 2 * b + 1) for b in range(bands - 1)] + [(1, 0)]
     piece = call(
         pack_kernel,
-        pltpu.VMEM((channels, half), BF16),
+        pltpu.VMEM((8, channels * half // 8), BF16),
         [HBM, HBM],
         61,
         1 << 20,
         (band_points, grid_field),
-        [pltpu.SMEM((1,), jnp.int32), pltpu.SemaphoreType.DMA, pltpu.SemaphoreType.DMA((8,))],
+        [
+            pltpu.VMEM((channels, half), BF16),
+            pltpu.SMEM((1,), jnp.int32),
+            pltpu.SemaphoreType.DMA,
+            pltpu.SemaphoreType.DMA((8,)),
+        ],
     )
     halo = lax.ppermute(piece, ("band", "ch"), pairs)
 
@@ -263,6 +308,14 @@
         16,
         8 * remap_flops,
         (block_ids, block_count, band_points, weight, grid_field),
+    )
+    from_hot, to_hot = call(
+        hots_kernel,
+        (shape((nodes, edges), BF16), shape((nodes, edges), BF16)),
+        [VMEM] * 2,
+        4,
+        edges * nodes * 16,
+        (src, dst),
     )
     into_edge, direct, agg, last = call(
         weights_kernel,
@@ -290,7 +343,7 @@
     )
 
     partial = call(
-        halo_kernel,
+        functools.partial(halo_kernel, channels),
         sums,
         [SMEM] * 2 + [VMEM] * 3,
         12,
@@ -299,15 +352,27 @@
         [pltpu.SMEM((2, kblocks), jnp.int32)],
     )
     mid = (partial + partner(partial)).astype(BF16)
-    near = lax.ppermute(mid, ("band", "ch"), pairs)
-    near_other = partner(near)
+
+    def exchange(first):
+        ups = [(b, (b + 1) % bands) for b in range(first, bands, 2)]
+        return lax.ppermute(mid, "band", ups + [(t, s) for s, t in ups])
+
+    far, near = exchange(1), exchange(0)
+    gathered = call(
+        gather_kernel,
+        shape((2 * rows, edges), BF16),
+        [VMEM] * 4,
+        8,
+        2 * edges * nodes * rows * 2,
+        (mid, src, from_hot, to_hot),
+    )
     by_node = call(
         edge_kernel,
         shape((nodes, share), BF16),
-        [VMEM] * 6,
+        [VMEM] * 7,
         24,
         2 * edges * nodes * 7 * 256,
-        (near, near_other, mid, into_edge, src, dst),
+        (near, far, into_edge, src, from_hot, to_hot, gathered),
         [pltpu.VMEM((nodes, share), F32)],
     )
     return call(

time: 55.8 us -> 52.8 us (0.946)
  the two profiles are of different devices: /device:TPU:129 before, /device:TPU:1 now
where the time goes in v1:
time: 52.8 us; the launch traced here: 52.6 us
  Pallas kernels  15.8 us (30%)
  starting transfers between devices  15.3 us (29%)
  waiting for transfers between devices  14.5 us (27%)
  local copies, waits for them, and re-layouts  5.46 us (10%)
  between operations  1.51 us (3%)
    pallas_call x8, Pallas kernels, call(): pl.pallas_call(kernel, out_shape=out, in_specs=specs, out_specs=[VMEM] *...  15.8 us
    ppermute x1, waiting for transfers between devices, on_device(): halo = lax.ppermute(piece, ('band', 'ch'), pairs)  13.1 us
    ppermute x2, starting transfers between devices, exchange(): return lax.ppermute(mid, 'band', ups + [(t, s) for s, t in ups])  10.1 us
    unnamed x20, local copies, waits for them, and re-layouts  5.46 us
    ppermute x6, starting transfers between devices, partner(): return lax.ppermute(x, 'ch', [(0, 1), (1, 0)])  5.07 us
    ppermute x6, waiting for transfers between devices, partner(): return lax.ppermute(x, 'ch', [(0, 1), (1, 0)])  1.37 us
  transfers between devices with their start and end apart: 9, of which 3 were waited for; matrix products, arithmetic and copies ran while one was open for 0% of the time, Pallas kernels for 20%

profile of v1, /device:TPU:1, one launch (start us, length us, event | category | flops | bytes accessed | tf_op | source)
XLA Modules:
  0.0 52.6 jit_solution(2396548871296074501)
XLA Ops:
  0.0 3.2 %collective-permute-start.5 = (bf16[2,1024,512]{2,1,0:T(8,128)(2,1)}, bf16[2,1024,512]{2,1,0:T(8,128)(2,1)}, u32[]{:S(2)}, u32[]{:S(2)}) collective-permute-start(bf16[2,1024,512]{2,1,0:T(8,128)(2,1)} %node_own_ref.1), channel_id=1, source_target_pairs={{0,1},{1,0},{2,3},{3,2},{4,5},{5,4},{6,7},{7,6},{8,9},{9,8},{10,11... | collective-permute-start | bytes 6291464 | tf_op jit(solution)/shard_map/ppermute | solution.py:295
  3.9 1.7 %shard_map.118 = bf16[8,102400]{1,0:T(8,128)(2,1)S(1)} custom-call(s32[1]{0:T(128)S(6)} %copy.13.band_points_ref.limit_ref, bf16[100,16384]{1,0:T(8,128)(2,1)} %points_ref.3), custom_call_target="tpu_custom_call" | custom-call | flops 1048576 | bytes 1048576 | tf_op jit(solution)/shard_map/pallas_call | solution.py:241
  5.6 0.1 collective-permute-start
  5.8 0.5 collective-permute-start.7
  6.9 2.2 %copy-done = bf16[1,16,256,512]{3,2,1,0:T(8,128)(2,1)S(1)} copy-done((bf16[1,16,256,512]{3,2,1,0:T(8,128)(2,1)S(1)}, bf16[1,16,256,512]{3,2,1,0:T(8,128)(2,1)}, u32[]{:S(2)}) %copy-start) | copy-done | bytes 4194328
  9.1 2.0 %copy-done.1 = bf16[100,16384]{1,0:T(8,128)(2,1)S(1)} copy-done((bf16[100,16384]{1,0:T(8,128)(2,1)S(1)}, bf16[100,16384]{1,0:T(8,128)(2,1)}, u32[]{:S(2)}) %copy-start.1) | copy-done | bytes 3276824
  11.1 1.4 %shard_map.119.own_ref = f32[112,256]{1,0:T(8,128)S(1)} custom-call(s32[1,16]{1,0:T(1,128)S(1)} %copy-done.8, s32[1]{0:T(128)S(6)} %copy.14.count_ref, s32[1]{0:T(128)S(6)} %copy.13.band_points_ref.limit_ref, bf16[16,256,512]{2,1,0:T(8,128)(2,1)S(1)} %bitcast.3, bf16[100,16384]{1,0:T(8,128)(2,1)S(1)} %copy-done.1), custom_call_target="tpu_custom_call" | custom-call | flops 838860800 | bytes 1048576 | tf_op jit(solution)/shard_map/pallas_call | solution.py:241
  12.5 13.1 %collective-permute-done.points_ref = bf16[8,102400]{1,0:T(8,128)(2,1)S(1)} collective-permute-done((bf16[8,102400]{1,0:T(8,128)(2,1)S(1)}, bf16[8,102400]{1,0:T(8,128)(2,1)S(1)}, u32[]{:S(2)}, u32[]{:S(2)}) %collective-permute-start) | collective-permute-done | bytes 1638432 | tf_op jit(solution)/shard_map/ppermute | solution.py:292
  25.6 1.2 %shard_map.120 = f32[112,256]{1,0:T(8,128)S(1)} custom-call(s32[1,16]{1,0:T(1,128)S(1)} %copy-done.8, s32[1]{0:T(128)S(6)} %copy.14.count_ref, bf16[16,256,512]{2,1,0:T(8,128)(2,1)S(1)} %bitcast.4, bf16[8,102400]{1,0:T(8,128)(2,1)S(1)} %collective-permute-done.points_ref, f32[112,256]{1,0:T(8,128)S(1)} %shard_map.119.own_ref), custom_call_target="tpu_custom_call" | custom-call | flops 104857600 | bytes 1048576 | tf_op jit(solution)/shard_map/pallas_call | solution.py:241
  26.8 0.1 collective-permute-start.1
  26.9 0.5 collective-permute-start.4
  27.4 0.6 %shard_map.122 = (bf16[256,5120]{1,0:T(8,128)(2,1)S(1)}, bf16[256,5120]{1,0:T(8,128)(2,1)S(1)}) custom-call(s32[1,5120]{1,0:T(1,128)S(1)} %bitcast.5, s32[1,5120]{1,0:T(1,128)S(1)} %bitcast.8), custom_call_target="tpu_custom_call" | custom-call | flops 20971520 | bytes 1048576 | tf_op jit(solution)/shard_map/pallas_call | solution.py:241
  28.0 0.2 collective-permute-done.1
  28.2 9.9 %collective-permute-start.3 = (bf16[112,256]{1,0:T(8,128)(2,1)S(1)}, bf16[112,256]{1,0:T(8,128)(2,1)S(1)}, u32[]{:S(2)}, u32[]{:S(2)}) collective-permute-start(bf16[112,256]{1,0:T(8,128)(2,1)S(1)} %add_convert_fusion.mid_ref), channel_id=1, source_target_pairs={{2,4},{6,8},{10,12},{14,16},{18,20},{22,24},{26,28},{30,32},{34,36... | collective-permute-start | bytes 172040 | tf_op jit(solution)/shard_map/ppermute | solution.py:358
  38.1 0.9 %shard_map.123.gathered_ref = bf16[224,5120]{1,0:T(8,128)(2,1)S(1)} custom-call(bf16[112,256]{1,0:T(8,128)(2,1)S(1)} %add_convert_fusion.mid_ref, s32[1,5120]{1,0:T(1,128)S(1)} %bitcast.6, bf16[256,5120]{1,0:T(8,128)(2,1)S(1)} %get-tuple-element.12.from_ref, bf16[256,5120]{1,0:T(8,128)(2,1)S(1)} %get-tuple-element.13.to_ref), custom_call_target="tpu_custom_call" | custom-call | flops 587202560 | bytes 1048576 | tf_op jit(solution)/shard_map/pallas_call | solution.py:241
  39.0 0.3 collective-permute-start.2
  39.3 0.3 copy-done.2
  39.7 0.6 %copy-done.3 = bf16[2,1024,512]{2,1,0:T(8,128)(2,1)S(1)} copy-done((bf16[2,1024,512]{2,1,0:T(8,128)(2,1)S(1)}, bf16[2,1024,512]{2,1,0:T(8,128)(2,1)}, u32[]{:S(2)}) %copy-start.3) | copy-done | bytes 2097176
  40.3 0.3 copy-done.5
  40.6 4.7 %shard_map.121 = (bf16[224,512]{1,0:T(8,128)(2,1)S(1)}, bf16[112,1024]{1,0:T(8,128)(2,1)S(1)}, bf16[2,512,1024]{2,1,0:T(8,128)(2,1)S(1)}, bf16[2,512,512]{2,1,0:T(8,128)(2,1)S(1)}) custom-call(bf16[100,512]{1,0:T(8,128)(2,1)S(1)} %copy-done.6, bf16[100,512]{1,0:T(8,128)(2,1)S(1)} %collective-permute-done.4.embed_other_ref, ...), custom_call_target="tpu_custom_call" | custom-call | flops 2147483648 | bytes 1048576 | tf_op jit(solution)/shard_map/pallas_call | solution.py:241
  45.3 3.5 %shard_map.124.own_ref = bf16[256,512]{1,0:T(8,128)(2,1)S(1)} custom-call(bf16[112,256]{1,0:T(8,128)(2,1)S(1)} %collective-permute-done.2.near_ref, bf16[112,256]{1,0:T(8,128)(2,1)S(1)} %collective-permute-done.3.far_ref, bf16[224,512]{1,0:T(8,128)(2,1)S(1)} %get-tuple-element.11.into_ref, s32[1,5120]{1,0:T(1,128)S(1)} %bitcast.7, ...), custom_call_target="tpu_custom_call" | custom-call | flops 4697620480 | bytes 1048576 | tf_op jit(solution)/shard_map/pallas_call | solution.py:241
  48.8 0.7 %collective-permute-start.8 = (bf16[256,512]{1,0:T(8,128)(2,1)S(1)}, bf16[256,512]{1,0:T(8,128)(2,1)S(1)}, u32[]{:S(2)}, u32[]{:S(2)}) collective-permute-start(bf16[256,512]{1,0:T(8,128)(2,1)S(1)} %shard_map.124.own_ref), channel_id=1, source_target_pairs={{0,1},{1,0},{2,3},{3,2},{4,5},{5,4},{6,7},{7,6},{8,9},{9,8},{10,11... | collective-permute-start | bytes 786440 | tf_op jit(solution)/shard_map/ppermute | solution.py:295
  49.5 1.2 %collective-permute-done.8.other_ref = bf16[256,512]{1,0:T(8,128)(2,1)S(1)} collective-permute-done((bf16[256,512]{1,0:T(8,128)(2,1)S(1)}, bf16[256,512]{1,0:T(8,128)(2,1)S(1)}, u32[]{:S(2)}, u32[]{:S(2)}) %collective-permute-start.8) | collective-permute-done | bytes 262176 | tf_op jit(solution)/shard_map/ppermute | solution.py:295
  50.7 1.9 %shard_map.125 = bf16[256,512]{1,0:T(8,128)(2,1)} custom-call(bf16[256,512]{1,0:T(8,128)(2,1)S(1)} %shard_map.124.own_ref, bf16[256,512]{1,0:T(8,128)(2,1)S(1)} %collective-permute-done.8.other_ref, bf16[112,256]{1,0:T(8,128)(2,1)S(1)} %add_convert_fusion.mid_ref, bf16[112,1024]{1,0:T(8,128)(2,1)S(1)} %get-tuple-element.14.direct_ref, ...), custom_call_target="tpu_custom_call" | custom-call | flops 805306368 | bytes 1048576 | tf_op jit(solution)/shard_map/pallas_call | solution.py:241
  (23 shorter events, 0.2 us)
Async XLA Ops:
  0.0 39.3 %collective-permute-start.5 = (bf16[2,1024,512]{2,1,0:T(8,128)(2,1)}, bf16[2,1024,512]{2,1,0:T(8,128)(2,1)}, u32[]{:S(2)}, u32[]{:S(2)}) collective-permute-start(bf16[2,1024,512]{2,1,0:T(8,128)(2,1)} %node_own_ref.1), channel_id=1, source_target_pairs={{0,1},{1,0},{2,3},{3,2},{4,5},{5,4},{6,7},{7,6},{8,9},{9,8},{10,11... | collective-permute-start | bytes 6291464 | tf_op jit(solution)/shard_map/ppermute | solution.py:295
  3.9 1.9 %copy-start.4 = (bf16[512,1024]{1,0:T(8,128)(2,1)S(1)}, bf16[512,1024]{1,0:T(8,128)(2,1)}, u32[]{:S(2)}) copy-start(bf16[512,1024]{1,0:T(8,128)(2,1)} %out_own_ref.1) | copy-start | bytes 3145732
  3.9 3.1 %copy-start.8 = (s32[1,16]{1,0:T(1,128)S(1)}, s32[1,16]{1,0:T(1,128)}, u32[]{:S(2)}) copy-start(s32[1,16]{1,0:T(1,128)} %ids_ref.3) | copy-start | bytes 196
  5.6 20.1 %collective-permute-start = (bf16[8,102400]{1,0:T(8,128)(2,1)S(1)}, bf16[8,102400]{1,0:T(8,128)(2,1)S(1)}, u32[]{:S(2)}, u32[]{:S(2)}) collective-permute-start(bf16[8,102400]{1,0:T(8,128)(2,1)S(1)} %shard_map.118), channel_id=1, source_target_pairs={{0,2},{2,4},{4,6},{6,8},{8,10},{10,12},{12,14},{14,16},{16,18},{18... | collective-permute-start | bytes 4915208 | tf_op jit(solution)/shard_map/ppermute | solution.py:292
  5.7 33.6 %collective-permute-start.6 = (bf16[512,1024]{1,0:T(8,128)(2,1)S(1)}, bf16[512,1024]{1,0:T(8,128)(2,1)S(1)}, u32[]{:S(2)}, u32[]{:S(2)}) collective-permute-start(bf16[512,1024]{1,0:T(8,128)(2,1)S(1)} %copy-done.4), channel_id=1, source_target_pairs={{0,1},{1,0},{2,3},{3,2},{4,5},{5,4},{6,7},{7,6},{8,9},{9,8},{10,11... | collective-permute-start | bytes 3145736 | tf_op jit(solution)/shard_map/ppermute | solution.py:295
  5.8 33.5 %collective-permute-start.7 = (bf16[512,1024]{1,0:T(8,128)(2,1)}, bf16[512,1024]{1,0:T(8,128)(2,1)S(1)}, u32[]{:S(2)}, u32[]{:S(2)}) collective-permute-start(bf16[512,1024]{1,0:T(8,128)(2,1)} %last_own_hbm.1), channel_id=1, source_target_pairs={{0,1},{1,0},{2,3},{3,2},{4,5},{5,4},{6,7},{7,6},{8,9},{9,8},{10,11... | collective-permute-start | bytes 3145736 | tf_op jit(solution)/shard_map/ppermute | solution.py:295
  6.9 2.2 %copy-start = (bf16[1,16,256,512]{3,2,1,0:T(8,128)(2,1)S(1)}, bf16[1,16,256,512]{3,2,1,0:T(8,128)(2,1)}, u32[]{:S(2)}) copy-start(bf16[1,16,256,512]{3,2,1,0:T(8,128)(2,1)} %param.16) | copy-start | bytes 12582916
  9.1 2.0 %copy-start.1 = (bf16[100,16384]{1,0:T(8,128)(2,1)S(1)}, bf16[100,16384]{1,0:T(8,128)(2,1)}, u32[]{:S(2)}) copy-start(bf16[100,16384]{1,0:T(8,128)(2,1)} %points_ref.3) | copy-start | bytes 9830404
  12.5 14.4 %copy-start.6 = (bf16[100,512]{1,0:T(8,128)(2,1)S(1)}, bf16[100,512]{1,0:T(8,128)(2,1)}, u32[]{:S(2)}) copy-start(bf16[100,512]{1,0:T(8,128)(2,1)} %embed_ref.3) | copy-start | bytes 307204
  12.5 14.9 %copy-start.7 = (s32[5120]{0:T(1024)S(1)}, s32[5120]{0:T(1024)}, u32[]{:S(2)}) copy-start(s32[5120]{0:T(1024)} %param.18) | copy-start | bytes 61444
  12.5 14.9 %copy-start.9 = (s32[5120]{0:T(1024)S(1)}, s32[5120]{0:T(1024)}, u32[]{:S(2)}) copy-start(s32[5120]{0:T(1024)} %param.19) | copy-start | bytes 61444
  26.8 1.4 %collective-permute-start.1 = (f32[112,256]{1,0:T(8,128)S(1)}, f32[112,256]{1,0:T(8,128)S(1)}, u32[]{:S(2)}, u32[]{:S(2)}) collective-permute-start(f32[112,256]{1,0:T(8,128)S(1)} %shard_map.120), channel_id=1, source_target_pairs={{0,1},{1,0},{2,3},{3,2},{4,5},{5,4},{6,7},{7,6},{8,9},{9,8},{10,11... | collective-permute-start | bytes 344072 | tf_op jit(solution)/shard_map/ppermute | solution.py:295
  26.9 12.1 %collective-permute-start.4 = (bf16[100,512]{1,0:T(8,128)(2,1)S(1)}, bf16[100,512]{1,0:T(8,128)(2,1)S(1)}, u32[]{:S(2)}, u32[]{:S(2)}) collective-permute-start(bf16[100,512]{1,0:T(8,128)(2,1)S(1)} %copy-done.6), channel_id=1, source_target_pairs={{0,1},{1,0},{2,3},{3,2},{4,5},{5,4},{6,7},{7,6},{8,9},{9,8},{10,11... | collective-permute-start | bytes 307208 | tf_op jit(solution)/shard_map/ppermute | solution.py:295
  28.2 17.0 %collective-permute-start.3 = (bf16[112,256]{1,0:T(8,128)(2,1)S(1)}, bf16[112,256]{1,0:T(8,128)(2,1)S(1)}, u32[]{:S(2)}, u32[]{:S(2)}) collective-permute-start(bf16[112,256]{1,0:T(8,128)(2,1)S(1)} %add_convert_fusion.mid_ref), channel_id=1, source_target_pairs={{2,4},{6,8},{10,12},{14,16},{18,20},{22,24},{26,28},{30,32},{34,36... | collective-permute-start | bytes 172040 | tf_op jit(solution)/shard_map/ppermute | solution.py:358
  38.1 1.6 %copy-start.2 = (bf16[2,1024,512]{2,1,0:T(8,128)(2,1)S(1)}, bf16[2,1024,512]{2,1,0:T(8,128)(2,1)}, u32[]{:S(2)}) copy-start(bf16[2,1024,512]{2,1,0:T(8,128)(2,1)} %edge_in_ref.1) | copy-start | bytes 6291460
  38.1 2.2 %copy-start.3 = (bf16[2,1024,512]{2,1,0:T(8,128)(2,1)S(1)}, bf16[2,1024,512]{2,1,0:T(8,128)(2,1)}, u32[]{:S(2)}) copy-start(bf16[2,1024,512]{2,1,0:T(8,128)(2,1)} %node_own_ref.1) | copy-start | bytes 6291460
  38.1 2.5 %copy-start.5 = (bf16[512,1024]{1,0:T(8,128)(2,1)S(1)}, bf16[512,1024]{1,0:T(8,128)(2,1)}, u32[]{:S(2)}) copy-start(bf16[512,1024]{1,0:T(8,128)(2,1)} %last_own_hbm.1) | copy-start | bytes 3145732
  39.0 6.3 %collective-permute-start.2 = (bf16[112,256]{1,0:T(8,128)(2,1)S(1)}, bf16[112,256]{1,0:T(8,128)(2,1)S(1)}, u32[]{:S(2)}, u32[]{:S(2)}) collective-permute-start(bf16[112,256]{1,0:T(8,128)(2,1)S(1)} %add_convert_fusion.mid_ref), channel_id=1, source_target_pairs={{0,2},{4,6},{8,10},{12,14},{16,18},{20,22},{24,26},{28,30},{32,34}... | collective-permute-start | bytes 172040 | tf_op jit(solution)/shard_map/ppermute | solution.py:358
  48.8 1.9 %collective-permute-start.8 = (bf16[256,512]{1,0:T(8,128)(2,1)S(1)}, bf16[256,512]{1,0:T(8,128)(2,1)S(1)}, u32[]{:S(2)}, u32[]{:S(2)}) collective-permute-start(bf16[256,512]{1,0:T(8,128)(2,1)S(1)} %shard_map.124.own_ref), channel_id=1, source_target_pairs={{0,1},{1,0},{2,3},{3,2},{4,5},{5,4},{6,7},{7,6},{8,9},{9,8},{10,11... | collective-permute-start | bytes 786440 | tf_op jit(solution)/shard_map/ppermute | solution.py:295

commit v2 on v1

--- a/solution.py
+++ b/solution.py
@@ -354,8 +354,11 @@
     mid = (partial + partner(partial)).astype(BF16)
 
     def exchange(first):
-        ups = [(b, (b + 1) % bands) for b in range(first, bands, 2)]
-        return lax.ppermute(mid, "band", ups + [(t, s) for s, t in ups])
+        ups = [(b, b + 1) for b in range(first, bands - 1, 2)]
+        moves = [(2 * x + c, 2 * y + c) for b, t in ups for x, y in ((b, t), (t, b)) for c in (0, 1)]
+        alone = set(range(bands)) - {b for up in ups for b in up}
+        moves += [(2 * b + c, 2 * b + 1 - c) for b in sorted(alone) for c in (0, 1)]
+        return lax.ppermute(mid, ("band", "ch"), moves)
 
     far, near = exchange(1), exchange(0)
     gathered = call(

time: 52.8 us -> 50.7 us (0.960)
  the two profiles are of different devices: /device:TPU:1 before, /device:TPU:129 now
where the time goes in v2:
time: 50.7 us; the launch traced here: 50.4 us
  Pallas kernels  15.4 us (30%)
  starting transfers between devices  15 us (30%)
  waiting for transfers between devices  13.2 us (26%)
  local copies, waits for them, and re-layouts  5.42 us (11%)
  between operations  1.48 us (3%)
    pallas_call x8, Pallas kernels, call(): pl.pallas_call(kernel, out_shape=out, in_specs=specs, out_specs=[VMEM] *...  15.4 us
    ppermute x1, waiting for transfers between devices, on_device(): halo = lax.ppermute(piece, ('band', 'ch'), pairs)  11.8 us
    ppermute x6, starting transfers between devices, partner(): return lax.ppermute(x, 'ch', [(0, 1), (1, 0)])  5.91 us
    unnamed x20, local copies, waits for them, and re-layouts  5.42 us
    ppermute x1, starting transfers between devices, on_device(): halo = lax.ppermute(piece, ('band', 'ch'), pairs)  4.55 us
    ppermute x2, starting transfers between devices, exchange(): return lax.ppermute(mid, ('band', 'ch'), moves)  4.5 us
    ppermute x6, waiting for transfers between devices, partner(): return lax.ppermute(x, 'ch', [(0, 1), (1, 0)])  1.41 us
  transfers between devices with their start and end apart: 9, of which 3 were waited for; matrix products, arithmetic and copies ran while one was open for 0% of the time, Pallas kernels for 20%

profile of v2, /device:TPU:129, one launch (start us, length us, event | category | flops | bytes accessed | tf_op | source)
XLA Modules:
  0.0 50.4 jit_solution(16607687831907071036)
XLA Ops:
  0.0 0.7 %collective-permute-start.5 = (bf16[2,1024,512]{2,1,0:T(8,128)(2,1)}, bf16[2,1024,512]{2,1,0:T(8,128)(2,1)}, u32[]{:S(2)}, u32[]{:S(2)}) collective-permute-start(bf16[2,1024,512]{2,1,0:T(8,128)(2,1)} %node_own_ref.1), channel_id=1, source_target_pairs={{0,1},{1,0},{2,3},{3,2},{4,5},{5,4},{6,7},{7,6},{8,9},{9,8},{10,11... | collective-permute-start | bytes 6291464 | tf_op jit(solution)/shard_map/ppermute | solution.py:295
  1.3 1.7 %shard_map.118 = bf16[8,102400]{1,0:T(8,128)(2,1)S(1)} custom-call(s32[1]{0:T(128)S(6)} %copy.13.band_points_ref.limit_ref, bf16[100,16384]{1,0:T(8,128)(2,1)} %points_ref.3), custom_call_target="tpu_custom_call" | custom-call | flops 1048576 | bytes 1048576 | tf_op jit(solution)/shard_map/pallas_call | solution.py:241
  3.0 4.5 %collective-permute-start = (bf16[8,102400]{1,0:T(8,128)(2,1)S(1)}, bf16[8,102400]{1,0:T(8,128)(2,1)S(1)}, u32[]{:S(2)}, u32[]{:S(2)}) collective-permute-start(bf16[8,102400]{1,0:T(8,128)(2,1)S(1)} %shard_map.118), channel_id=1, source_target_pairs={{0,2},{2,4},{4,6},{6,8},{8,10},{10,12},{12,14},{14,16},{16,18},{18... | collective-permute-start | bytes 4915208 | tf_op jit(solution)/shard_map/ppermute | solution.py:292
  7.6 0.5 %collective-permute-start.7 = (bf16[512,1024]{1,0:T(8,128)(2,1)}, bf16[512,1024]{1,0:T(8,128)(2,1)S(1)}, u32[]{:S(2)}, u32[]{:S(2)}) collective-permute-start(bf16[512,1024]{1,0:T(8,128)(2,1)} %last_own_hbm.1), channel_id=1, source_target_pairs={{0,1},{1,0},{2,3},{3,2},{4,5},{5,4},{6,7},{7,6},{8,9},{9,8},{10,11... | collective-permute-start | bytes 3145736 | tf_op jit(solution)/shard_map/ppermute | solution.py:295
  8.8 2.2 %copy-done = bf16[1,16,256,512]{3,2,1,0:T(8,128)(2,1)S(1)} copy-done((bf16[1,16,256,512]{3,2,1,0:T(8,128)(2,1)S(1)}, bf16[1,16,256,512]{3,2,1,0:T(8,128)(2,1)}, u32[]{:S(2)}) %copy-start) | copy-done | bytes 4194328
  11.0 2.0 %copy-done.1 = bf16[100,16384]{1,0:T(8,128)(2,1)S(1)} copy-done((bf16[100,16384]{1,0:T(8,128)(2,1)S(1)}, bf16[100,16384]{1,0:T(8,128)(2,1)}, u32[]{:S(2)}) %copy-start.1) | copy-done | bytes 3276824
  12.9 0.9 %shard_map.119.own_ref = f32[112,256]{1,0:T(8,128)S(1)} custom-call(s32[1,16]{1,0:T(1,128)S(1)} %copy-done.8, s32[1]{0:T(128)S(6)} %copy.14.count_ref, s32[1]{0:T(128)S(6)} %copy.13.band_points_ref.limit_ref, bf16[16,256,512]{2,1,0:T(8,128)(2,1)S(1)} %bitcast.3, bf16[100,16384]{1,0:T(8,128)(2,1)S(1)} %copy-done.1), custom_call_target="tpu_custom_call" | custom-call | flops 838860800 | bytes 1048576 | tf_op jit(solution)/shard_map/pallas_call | solution.py:241
  13.9 11.8 %collective-permute-done.points_ref = bf16[8,102400]{1,0:T(8,128)(2,1)S(1)} collective-permute-done((bf16[8,102400]{1,0:T(8,128)(2,1)S(1)}, bf16[8,102400]{1,0:T(8,128)(2,1)S(1)}, u32[]{:S(2)}, u32[]{:S(2)}) %collective-permute-start) | collective-permute-done | bytes 1638432 | tf_op jit(solution)/shard_map/ppermute | solution.py:292
  25.7 1.2 %shard_map.120 = f32[112,256]{1,0:T(8,128)S(1)} custom-call(s32[1,16]{1,0:T(1,128)S(1)} %copy-done.8, s32[1]{0:T(128)S(6)} %copy.14.count_ref, bf16[16,256,512]{2,1,0:T(8,128)(2,1)S(1)} %bitcast.4, bf16[8,102400]{1,0:T(8,128)(2,1)S(1)} %collective-permute-done.points_ref, f32[112,256]{1,0:T(8,128)S(1)} %shard_map.119.own_ref), custom_call_target="tpu_custom_call" | custom-call | flops 104857600 | bytes 1048576 | tf_op jit(solution)/shard_map/pallas_call | solution.py:241
  26.8 4.1 %collective-permute-start.1 = (f32[112,256]{1,0:T(8,128)S(1)}, f32[112,256]{1,0:T(8,128)S(1)}, u32[]{:S(2)}, u32[]{:S(2)}) collective-permute-start(f32[112,256]{1,0:T(8,128)S(1)} %shard_map.120), channel_id=1, source_target_pairs={{0,1},{1,0},{2,3},{3,2},{4,5},{5,4},{6,7},{7,6},{8,9},{9,8},{10,11... | collective-permute-start | bytes 344072 | tf_op jit(solution)/shard_map/ppermute | solution.py:295
  30.9 0.1 collective-permute-start.4
  31.1 0.6 %shard_map.122 = (bf16[256,5120]{1,0:T(8,128)(2,1)S(1)}, bf16[256,5120]{1,0:T(8,128)(2,1)S(1)}) custom-call(s32[1,5120]{1,0:T(1,128)S(1)} %bitcast.5, s32[1,5120]{1,0:T(1,128)S(1)} %bitcast.8), custom_call_target="tpu_custom_call" | custom-call | flops 20971520 | bytes 1048576 | tf_op jit(solution)/shard_map/pallas_call | solution.py:241
  31.7 0.2 collective-permute-done.1
  31.9 4.2 %collective-permute-start.3 = (bf16[112,256]{1,0:T(8,128)(2,1)S(1)}, bf16[112,256]{1,0:T(8,128)(2,1)S(1)}, u32[]{:S(2)}, u32[]{:S(2)}) collective-permute-start(bf16[112,256]{1,0:T(8,128)(2,1)S(1)} %add_convert_fusion.mid_ref), channel_id=1, source_target_pairs={{2,4},{3,5},{4,2},{5,3},{6,8},{7,9},{8,6},{9,7},{10,12},{11,13},{1... | collective-permute-start | bytes 172040 | tf_op jit(solution)/shard_map/ppermute | solution.py:361
  36.2 0.9 %shard_map.123.gathered_ref = bf16[224,5120]{1,0:T(8,128)(2,1)S(1)} custom-call(bf16[112,256]{1,0:T(8,128)(2,1)S(1)} %add_convert_fusion.mid_ref, s32[1,5120]{1,0:T(1,128)S(1)} %bitcast.6, bf16[256,5120]{1,0:T(8,128)(2,1)S(1)} %get-tuple-element.12.from_ref, bf16[256,5120]{1,0:T(8,128)(2,1)S(1)} %get-tuple-element.13.to_ref), custom_call_target="tpu_custom_call" | custom-call | flops 587202560 | bytes 1048576 | tf_op jit(solution)/shard_map/pallas_call | solution.py:241
  37.1 0.3 collective-permute-start.2
  37.4 0.3 copy-done.2
  37.7 0.6 %copy-done.3 = bf16[2,1024,512]{2,1,0:T(8,128)(2,1)S(1)} copy-done((bf16[2,1024,512]{2,1,0:T(8,128)(2,1)S(1)}, bf16[2,1024,512]{2,1,0:T(8,128)(2,1)}, u32[]{:S(2)}) %copy-start.3) | copy-done | bytes 2097176
  38.4 0.3 copy-done.5
  38.6 4.7 %shard_map.121 = (bf16[224,512]{1,0:T(8,128)(2,1)S(1)}, bf16[112,1024]{1,0:T(8,128)(2,1)S(1)}, bf16[2,512,1024]{2,1,0:T(8,128)(2,1)S(1)}, bf16[2,512,512]{2,1,0:T(8,128)(2,1)S(1)}) custom-call(bf16[100,512]{1,0:T(8,128)(2,1)S(1)} %copy-done.6, bf16[100,512]{1,0:T(8,128)(2,1)S(1)} %collective-permute-done.4.embed_other_ref, ...), custom_call_target="tpu_custom_call" | custom-call | flops 2147483648 | bytes 1048576 | tf_op jit(solution)/shard_map/pallas_call | solution.py:241
  43.3 3.5 %shard_map.124.own_ref = bf16[256,512]{1,0:T(8,128)(2,1)S(1)} custom-call(bf16[112,256]{1,0:T(8,128)(2,1)S(1)} %collective-permute-done.2.near_ref, bf16[112,256]{1,0:T(8,128)(2,1)S(1)} %collective-permute-done.3.far_ref, bf16[224,512]{1,0:T(8,128)(2,1)S(1)} %get-tuple-element.11.into_ref, s32[1,5120]{1,0:T(1,128)S(1)} %bitcast.7, ...), custom_call_target="tpu_custom_call" | custom-call | flops 4697620480 | bytes 1048576 | tf_op jit(solution)/shard_map/pallas_call | solution.py:241
  46.9 0.5 %collective-permute-start.8 = (bf16[256,512]{1,0:T(8,128)(2,1)S(1)}, bf16[256,512]{1,0:T(8,128)(2,1)S(1)}, u32[]{:S(2)}, u32[]{:S(2)}) collective-permute-start(bf16[256,512]{1,0:T(8,128)(2,1)S(1)} %shard_map.124.own_ref), channel_id=1, source_target_pairs={{0,1},{1,0},{2,3},{3,2},{4,5},{5,4},{6,7},{7,6},{8,9},{9,8},{10,11... | collective-permute-start | bytes 786440 | tf_op jit(solution)/shard_map/ppermute | solution.py:295
  47.4 1.2 %collective-permute-done.8.other_ref = bf16[256,512]{1,0:T(8,128)(2,1)S(1)} collective-permute-done((bf16[256,512]{1,0:T(8,128)(2,1)S(1)}, bf16[256,512]{1,0:T(8,128)(2,1)S(1)}, u32[]{:S(2)}, u32[]{:S(2)}) %collective-permute-start.8) | collective-permute-done | bytes 262176 | tf_op jit(solution)/shard_map/ppermute | solution.py:295
  48.5 1.9 %shard_map.125 = bf16[256,512]{1,0:T(8,128)(2,1)} custom-call(bf16[256,512]{1,0:T(8,128)(2,1)S(1)} %shard_map.124.own_ref, bf16[256,512]{1,0:T(8,128)(2,1)S(1)} %collective-permute-done.8.other_ref, bf16[112,256]{1,0:T(8,128)(2,1)S(1)} %add_convert_fusion.mid_ref, bf16[112,1024]{1,0:T(8,128)(2,1)S(1)} %get-tuple-element.14.direct_ref, ...), custom_call_target="tpu_custom_call" | custom-call | flops 805306368 | bytes 1048576 | tf_op jit(solution)/shard_map/pallas_call | solution.py:241
  (23 shorter events, 0.1 us)
Async XLA Ops:
  0.0 37.4 %collective-permute-start.5 = (bf16[2,1024,512]{2,1,0:T(8,128)(2,1)}, bf16[2,1024,512]{2,1,0:T(8,128)(2,1)}, u32[]{:S(2)}, u32[]{:S(2)}) collective-permute-start(bf16[2,1024,512]{2,1,0:T(8,128)(2,1)} %node_own_ref.1), channel_id=1, source_target_pairs={{0,1},{1,0},{2,3},{3,2},{4,5},{5,4},{6,7},{7,6},{8,9},{9,8},{10,11... | collective-permute-start | bytes 6291464 | tf_op jit(solution)/shard_map/ppermute | solution.py:295
  1.3 6.3 %copy-start.4 = (bf16[512,1024]{1,0:T(8,128)(2,1)S(1)}, bf16[512,1024]{1,0:T(8,128)(2,1)}, u32[]{:S(2)}) copy-start(bf16[512,1024]{1,0:T(8,128)(2,1)} %out_own_ref.1) | copy-start | bytes 3145732
  1.3 7.4 %copy-start.8 = (s32[1,16]{1,0:T(1,128)S(1)}, s32[1,16]{1,0:T(1,128)}, u32[]{:S(2)}) copy-start(s32[1,16]{1,0:T(1,128)} %ids_ref.3) | copy-start | bytes 196
  3.0 22.6 %collective-permute-start = (bf16[8,102400]{1,0:T(8,128)(2,1)S(1)}, bf16[8,102400]{1,0:T(8,128)(2,1)S(1)}, u32[]{:S(2)}, u32[]{:S(2)}) collective-permute-start(bf16[8,102400]{1,0:T(8,128)(2,1)S(1)} %shard_map.118), channel_id=1, source_target_pairs={{0,2},{2,4},{4,6},{6,8},{8,10},{10,12},{12,14},{14,16},{16,18},{18... | collective-permute-start | bytes 4915208 | tf_op jit(solution)/shard_map/ppermute | solution.py:292
  7.6 29.8 %collective-permute-start.6 = (bf16[512,1024]{1,0:T(8,128)(2,1)S(1)}, bf16[512,1024]{1,0:T(8,128)(2,1)S(1)}, u32[]{:S(2)}, u32[]{:S(2)}) collective-permute-start(bf16[512,1024]{1,0:T(8,128)(2,1)S(1)} %copy-done.4), channel_id=1, source_target_pairs={{0,1},{1,0},{2,3},{3,2},{4,5},{5,4},{6,7},{7,6},{8,9},{9,8},{10,11... | collective-permute-start | bytes 3145736 | tf_op jit(solution)/shard_map/ppermute | solution.py:295
  7.6 29.8 %collective-permute-start.7 = (bf16[512,1024]{1,0:T(8,128)(2,1)}, bf16[512,1024]{1,0:T(8,128)(2,1)S(1)}, u32[]{:S(2)}, u32[]{:S(2)}) collective-permute-start(bf16[512,1024]{1,0:T(8,128)(2,1)} %last_own_hbm.1), channel_id=1, source_target_pairs={{0,1},{1,0},{2,3},{3,2},{4,5},{5,4},{6,7},{7,6},{8,9},{9,8},{10,11... | collective-permute-start | bytes 3145736 | tf_op jit(solution)/shard_map/ppermute | solution.py:295
  8.8 2.2 %copy-start = (bf16[1,16,256,512]{3,2,1,0:T(8,128)(2,1)S(1)}, bf16[1,16,256,512]{3,2,1,0:T(8,128)(2,1)}, u32[]{:S(2)}) copy-start(bf16[1,16,256,512]{3,2,1,0:T(8,128)(2,1)} %param.16) | copy-start | bytes 12582916
  11.0 2.0 %copy-start.1 = (bf16[100,16384]{1,0:T(8,128)(2,1)S(1)}, bf16[100,16384]{1,0:T(8,128)(2,1)}, u32[]{:S(2)}) copy-start(bf16[100,16384]{1,0:T(8,128)(2,1)} %points_ref.3) | copy-start | bytes 9830404
  13.9 17.1 %copy-start.6 = (bf16[100,512]{1,0:T(8,128)(2,1)S(1)}, bf16[100,512]{1,0:T(8,128)(2,1)}, u32[]{:S(2)}) copy-start(bf16[100,512]{1,0:T(8,128)(2,1)} %embed_ref.3) | copy-start | bytes 307204
  13.9 17.2 %copy-start.7 = (s32[5120]{0:T(1024)S(1)}, s32[5120]{0:T(1024)}, u32[]{:S(2)}) copy-start(s32[5120]{0:T(1024)} %param.18) | copy-start | bytes 61444
  13.9 17.2 %copy-start.9 = (s32[5120]{0:T(1024)S(1)}, s32[5120]{0:T(1024)}, u32[]{:S(2)}) copy-start(s32[5120]{0:T(1024)} %param.19) | copy-start | bytes 61444
  26.8 5.1 %collective-permute-start.1 = (f32[112,256]{1,0:T(8,128)S(1)}, f32[112,256]{1,0:T(8,128)S(1)}, u32[]{:S(2)}, u32[]{:S(2)}) collective-permute-start(f32[112,256]{1,0:T(8,128)S(1)} %shard_map.120), channel_id=1, source_target_pairs={{0,1},{1,0},{2,3},{3,2},{4,5},{5,4},{6,7},{7,6},{8,9},{9,8},{10,11... | collective-permute-start | bytes 344072 | tf_op jit(solution)/shard_map/ppermute | solution.py:295
  30.9 6.1 %collective-permute-start.4 = (bf16[100,512]{1,0:T(8,128)(2,1)S(1)}, bf16[100,512]{1,0:T(8,128)(2,1)S(1)}, u32[]{:S(2)}, u32[]{:S(2)}) collective-permute-start(bf16[100,512]{1,0:T(8,128)(2,1)S(1)} %copy-done.6), channel_id=1, source_target_pairs={{0,1},{1,0},{2,3},{3,2},{4,5},{5,4},{6,7},{7,6},{8,9},{9,8},{10,11... | collective-permute-start | bytes 307208 | tf_op jit(solution)/shard_map/ppermute | solution.py:295
  31.9 11.4 %collective-permute-start.3 = (bf16[112,256]{1,0:T(8,128)(2,1)S(1)}, bf16[112,256]{1,0:T(8,128)(2,1)S(1)}, u32[]{:S(2)}, u32[]{:S(2)}) collective-permute-start(bf16[112,256]{1,0:T(8,128)(2,1)S(1)} %add_convert_fusion.mid_ref), channel_id=1, source_target_pairs={{2,4},{3,5},{4,2},{5,3},{6,8},{7,9},{8,6},{9,7},{10,12},{11,13},{1... | collective-permute-start | bytes 172040 | tf_op jit(solution)/shard_map/ppermute | solution.py:361
  36.1 1.6 %copy-start.2 = (bf16[2,1024,512]{2,1,0:T(8,128)(2,1)S(1)}, bf16[2,1024,512]{2,1,0:T(8,128)(2,1)}, u32[]{:S(2)}) copy-start(bf16[2,1024,512]{2,1,0:T(8,128)(2,1)} %edge_in_ref.1) | copy-start | bytes 6291460
  36.2 2.2 %copy-start.3 = (bf16[2,1024,512]{2,1,0:T(8,128)(2,1)S(1)}, bf16[2,1024,512]{2,1,0:T(8,128)(2,1)}, u32[]{:S(2)}) copy-start(bf16[2,1024,512]{2,1,0:T(8,128)(2,1)} %node_own_ref.1) | copy-start | bytes 6291460
  36.2 2.5 %copy-start.5 = (bf16[512,1024]{1,0:T(8,128)(2,1)S(1)}, bf16[512,1024]{1,0:T(8,128)(2,1)}, u32[]{:S(2)}) copy-start(bf16[512,1024]{1,0:T(8,128)(2,1)} %last_own_hbm.1) | copy-start | bytes 3145732
  37.1 6.3 %collective-permute-start.2 = (bf16[112,256]{1,0:T(8,128)(2,1)S(1)}, bf16[112,256]{1,0:T(8,128)(2,1)S(1)}, u32[]{:S(2)}, u32[]{:S(2)}) collective-permute-start(bf16[112,256]{1,0:T(8,128)(2,1)S(1)} %add_convert_fusion.mid_ref), channel_id=1, source_target_pairs={{0,2},{1,3},{2,0},{3,1},{4,6},{5,7},{6,4},{7,5},{8,10},{9,11},{10,... | collective-permute-start | bytes 172040 | tf_op jit(solution)/shard_map/ppermute | solution.py:361
  46.9 1.7 %collective-permute-start.8 = (bf16[256,512]{1,0:T(8,128)(2,1)S(1)}, bf16[256,512]{1,0:T(8,128)(2,1)S(1)}, u32[]{:S(2)}, u32[]{:S(2)}) collective-permute-start(bf16[256,512]{1,0:T(8,128)(2,1)S(1)} %shard_map.124.own_ref), channel_id=1, source_target_pairs={{0,1},{1,0},{2,3},{3,2},{4,5},{5,4},{6,7},{7,6},{8,9},{9,8},{10,11... | collective-permute-start | bytes 786440 | tf_op jit(solution)/shard_map/ppermute | solution.py:295

commit v3 on v2

--- a/solution.py
+++ b/solution.py
@@ -20,16 +20,16 @@
     return v * (0.5 * jnp.tanh(0.5 * v) + 0.5)
 
 
-def pack_kernel(band_points_ref, points_ref, out_ref, rows_ref, limit_ref, limit_sem, sems):
+def pack_kernel(half, offset, band_points_ref, points_ref, out_ref, rows_ref, limit_ref, limit_sem, sems):
     core = lax.axis_index("ch")
-    channels, half = rows_ref.shape
+    channels, run = rows_ref.shape
     parts = sems.shape[0]
-    width = half // parts
+    width = run // parts
     limit_copy = pltpu.make_async_copy(band_points_ref, limit_ref, limit_sem)
     limit_copy.start()
     copies = []
     for i in range(parts):
-        start = pl.multiple_of((1 - core) * half + i * width, width)
+        start = pl.multiple_of((1 - core) * half + offset + i * width, width)
         copies.append(
             pltpu.make_async_copy(
                 points_ref.at[:, pl.ds(start, width)],
@@ -39,7 +39,7 @@
         )
         copies[-1].start()
     limit_copy.wait()
-    limit = jnp.where(core == 0, limit_ref[0] - half, half)
+    limit = jnp.where(core == 0, limit_ref[0] - half, half) - offset
     full = channels // 8
     last = channels - 8 * full
     for i in range(parts):
@@ -48,12 +48,12 @@
         live = at + lax.broadcasted_iota(jnp.int32, (8, width), 1) < limit
         for t in range(full):
             x = rows_ref[8 * t : 8 * t + 8, at : at + width]
-            out_ref[:, t * half + at : t * half + at + width] = jnp.where(live, x, jnp.zeros_like(x))
+            out_ref[:, t * run + at : t * run + at + width] = jnp.where(live, x, jnp.zeros_like(x))
         x = rows_ref[8 * full :, at : at + width]
         x = jnp.where(live[:last], x, jnp.zeros_like(x))
-        low = at % (half * last // 8)
-        row = (at // (half * last // 8)) * last
-        out_ref[row : row + last, full * half + low : full * half + low + width] = x
+        low = at % (run * last // 8)
+        row = (at // (run * last // 8)) * last
+        out_ref[row : row + last, full * run + low : full * run + low + width] = x
 
 
 def own_kernel(
@@ -106,14 +106,26 @@
         out_ref[rows:, at : at + size] = got.astype(BF16)
 
 
-def halo_kernel(channels, ids_ref, count_ref, weight_ref, points_ref, own_ref, out_ref, slots):
+def halo_kernel(channels, ids_ref, count_ref, weight_ref, early_ref, late_ref, own_ref, out_ref, slots):
     band, core = lax.axis_index("band"), lax.axis_index("ch")
     kblocks, _, block_len = weight_ref.shape
-    half = points_ref.shape[1] * 8 // channels
-    blocks = half // block_len
+    runs = [ref.shape[1] * 8 // channels for ref in (early_ref, late_ref)]
+    blocks = sum(runs) // block_len
     sub_count = 2 * blocks
     full = channels // 8
     last = channels - 8 * full
+
+    def rows_of(ref, run, at):
+        x = [
+            ref[:, pl.ds(pl.multiple_of(t * run + at, block_len), block_len)].astype(F32)
+            for t in range(full)
+        ]
+        stack = run * last // 8
+        low = pl.multiple_of(full * run + lax.rem(at, stack), block_len)
+        tail = ref[:, pl.ds(low, block_len)].astype(F32)
+        tail = jnp.where(at < stack, tail[:last], tail[last : 2 * last])
+        return jnp.concatenate(x + [tail], axis=0)
+
     found = jnp.int32(0)
     for k in range(kblocks):
         local = ids_ref[0, k] - band * sub_count
@@ -140,15 +152,11 @@
                 k = jnp.where(used, slots[0, j], 0)
                 block = jnp.where(used, slots[1, j], 0)
                 at = pl.multiple_of(block * block_len, block_len)
-                x = [
-                    points_ref[:, pl.ds(pl.multiple_of(t * half + at, block_len), block_len)]
-                    for t in range(full)
-                ]
-                stack = half * last // 8
-                low = pl.multiple_of(full * half + lax.rem(at, stack), block_len)
-                tail = points_ref[:, pl.ds(low, block_len)].astype(F32)
-                tail = jnp.where(at < stack, tail[:last], tail[last : 2 * last])
-                x = jnp.concatenate([piece.astype(F32) for piece in x] + [tail], axis=0)
+                x = jnp.where(
+                    at < runs[0],
+                    rows_of(early_ref, runs[0], jnp.minimum(at, runs[0] - block_len)),
+                    rows_of(late_ref, runs[1], jnp.maximum(at - runs[0], 0)),
+                )
                 x = jnp.where(used, x, 0.0).astype(BF16)
                 part = lax.dot_general(x, weight_ref[k], NT, preferred_element_type=F32)
                 total = part if total is None else total + part
@@ -275,21 +283,26 @@
 
     pairs = [(2 * b, 2 * b + 2) for b in range(bands - 1)] + [(2 * bands - 2, 2 * bands - 1)]
     pairs += [(2 * b + 3, 2 * b + 1) for b in range(bands - 1)] + [(1, 0)]
-    piece = call(
-        pack_kernel,
-        pltpu.VMEM((8, channels * half // 8), BF16),
-        [HBM, HBM],
-        61,
-        1 << 20,
-        (band_points, grid_field),
-        [
-            pltpu.VMEM((channels, half), BF16),
-            pltpu.SMEM((1,), jnp.int32),
-            pltpu.SemaphoreType.DMA,
-            pltpu.SemaphoreType.DMA((8,)),
-        ],
-    )
-    halo = lax.ppermute(piece, ("band", "ch"), pairs)
+    split = 6 * block_len
+
+    def send(offset, run, limit):
+        piece = call(
+            functools.partial(pack_kernel, half, offset),
+            pltpu.VMEM((8, channels * run // 8), BF16),
+            [HBM, HBM],
+            limit,
+            1 << 20,
+            (band_points, grid_field),
+            [
+                pltpu.VMEM((channels, run), BF16),
+                pltpu.SMEM((1,), jnp.int32),
+                pltpu.SemaphoreType.DMA,
+                pltpu.SemaphoreType.DMA((run // block_len,)),
+            ],
+        )
+        return lax.ppermute(piece, ("band", "ch"), pairs)
+
+    early, late = send(0, split, 61), send(split, half - split, 40)
 
     def partner(x):
         return lax.ppermute(x, "ch", [(0, 1), (1, 0)])
@@ -345,10 +358,10 @@
     partial = call(
         functools.partial(halo_kernel, channels),
         sums,
-        [SMEM] * 2 + [VMEM] * 3,
+        [SMEM] * 2 + [VMEM] * 4,
         12,
         remap_flops,
-        (block_ids, block_count, weight, halo, partial),
+        (block_ids, block_count, weight, early, late, partial),
         [pltpu.SMEM((2, kblocks), jnp.int32)],
     )
     mid = (partial + partner(partial)).astype(BF16)

time: 50.7 us -> 54.2 us (1.069)
  waiting for transfers between devices: 13.2 us -> 9.87 us
  Pallas kernels: 15.4 us -> 18.2 us
  starting transfers between devices: 15 us -> 17.3 us
  local copies, waits for them, and re-layouts: 5.42 us -> 7.07 us
    ppermute x1 -> x2, waiting for transfers between devices: 11.8 us -> 8.45 us  [send(): return lax.ppermute(piece, ('band', 'ch'), pairs)]
    pallas_call x8 -> x9, Pallas kernels: 15.4 us -> 18.2 us  [call(): pl.pallas_call(kernel, out_shape=out, in_specs=specs, out_specs=[VMEM] *...]
    ppermute x1 -> x2, starting transfers between devices: 4.55 us -> 6.83 us  [send(): return lax.ppermute(piece, ('band', 'ch'), pairs)]
    unnamed x20 -> x18, local copies, waits for them, and re-layouts: 5.42 us -> 7.07 us
  transfers between devices with their start and end apart: 9 -> 10, of which waited for: 3 -> 3; matrix products, arithmetic and copies ran while one was open for 0% -> 0% of each run, Pallas kernels for 20% -> 23%
where the time goes in v3:
time: 54.2 us; the launch traced here: 53.9 us
  Pallas kernels  18.2 us (34%)
  starting transfers between devices  17.3 us (32%)
  waiting for transfers between devices  9.87 us (18%)
  local copies, waits for them, and re-layouts  7.07 us (13%)
  between operations  1.49 us (3%)
    pallas_call x9, Pallas kernels, call(): pl.pallas_call(kernel, out_shape=out, in_specs=specs, out_specs=[VMEM] *...  18.2 us
    ppermute x2, waiting for transfers between devices, send(): return lax.ppermute(piece, ('band', 'ch'), pairs)  8.45 us
    unnamed x18, local copies, waits for them, and re-layouts  7.07 us
    ppermute x2, starting transfers between devices, send(): return lax.ppermute(piece, ('band', 'ch'), pairs)  6.83 us
    ppermute x6, starting transfers between devices, partner(): return lax.ppermute(x, 'ch', [(0, 1), (1, 0)])  5.91 us
    ppermute x2, starting transfers between devices, exchange(): return lax.ppermute(mid, ('band', 'ch'), moves)  4.52 us
    ppermute x6, waiting for transfers between devices, partner(): return lax.ppermute(x, 'ch', [(0, 1), (1, 0)])  1.41 us
  transfers between devices with their start and end apart: 10, of which 3 were waited for; matrix products, arithmetic and copies ran while one was open for 0% of the time, Pallas kernels for 23%

profile of v3, /device:TPU:129, one launch (start us, length us, event | category | flops | bytes accessed | tf_op | source)
XLA Modules:
  0.0 53.9 jit_solution(18311145650162622782)
XLA Ops:
  0.0 0.7 %collective-permute-start.6 = (bf16[2,1024,512]{2,1,0:T(8,128)(2,1)}, bf16[2,1024,512]{2,1,0:T(8,128)(2,1)S(1)}, u32[]{:S(2)}, u32[]{:S(2)}) collective-permute-start(bf16[2,1024,512]{2,1,0:T(8,128)(2,1)} %node_own_ref.1), channel_id=1, source_target_pairs={{0,1},{1,0},{2,3},{3,2},{4,5},{5,4},{6,7},{7,6},{8,9},{9,8},{10,11... | collective-permute-start | bytes 6291464 | tf_op jit(solution)/shard_map/ppermute | solution.py:308
  1.3 2.0 %copy-done = bf16[100,16384]{1,0:T(8,128)(2,1)S(1)} copy-done((bf16[100,16384]{1,0:T(8,128)(2,1)S(1)}, bf16[100,16384]{1,0:T(8,128)(2,1)}, u32[]{:S(2)}) %copy-start) | copy-done | bytes 3276824
  3.3 1.7 %shard_map.119 = bf16[8,64000]{1,0:T(8,128)(2,1)} custom-call(s32[1]{0:T(128)S(6)} %copy.13.band_points_ref.limit_ref, bf16[100,16384]{1,0:T(8,128)(2,1)S(1)} %copy-done), custom_call_target="tpu_custom_call" | custom-call | flops 1048576 | bytes 1048576 | tf_op jit(solution)/shard_map/pallas_call | solution.py:249
  5.0 4.5 %collective-permute-start.1 = (bf16[8,64000]{1,0:T(8,128)(2,1)}, bf16[8,64000]{1,0:T(8,128)(2,1)}, u32[]{:S(2)}, u32[]{:S(2)}) collective-permute-start(bf16[8,64000]{1,0:T(8,128)(2,1)} %shard_map.119), channel_id=1, source_target_pairs={{0,2},{2,4},{4,6},{6,8},{8,10},{10,12},{12,14},{14,16},{16,18},{18... | collective-permute-start | bytes 3072008 | tf_op jit(solution)/shard_map/ppermute | solution.py:303
  9.6 0.5 collective-permute-start.8
  10.1 1.2 %shard_map.118 = bf16[8,38400]{1,0:T(8,128)(2,1)S(1)} custom-call(s32[1]{0:T(128)S(6)} %copy.13.band_points_ref.limit_ref, bf16[100,16384]{1,0:T(8,128)(2,1)} %points_ref.5), custom_call_target="tpu_custom_call" | custom-call | flops 1048576 | bytes 1048576 | tf_op jit(solution)/shard_map/pallas_call | solution.py:249
  11.3 2.3 %collective-permute-start = (bf16[8,38400]{1,0:T(8,128)(2,1)S(1)}, bf16[8,38400]{1,0:T(8,128)(2,1)S(1)}, u32[]{:S(2)}, u32[]{:S(2)}) collective-permute-start(bf16[8,38400]{1,0:T(8,128)(2,1)S(1)} %shard_map.118), channel_id=1, source_target_pairs={{0,2},{2,4},{4,6},{6,8},{8,10},{10,12},{12,14},{14,16},{16,18},{18... | collective-permute-start | bytes 1843208 | tf_op jit(solution)/shard_map/ppermute | solution.py:303
  14.3 2.0 %copy-done.1 = bf16[100,16384]{1,0:T(8,128)(2,1)S(1)} copy-done((bf16[100,16384]{1,0:T(8,128)(2,1)S(1)}, bf16[100,16384]{1,0:T(8,128)(2,1)}, u32[]{:S(2)}) %copy-start.1) | copy-done | bytes 3276824
  16.2 2.2 %copy-done.2 = bf16[1,16,256,512]{3,2,1,0:T(8,128)(2,1)S(1)} copy-done((bf16[1,16,256,512]{3,2,1,0:T(8,128)(2,1)S(1)}, bf16[1,16,256,512]{3,2,1,0:T(8,128)(2,1)}, u32[]{:S(2)}) %copy-start.2) | copy-done | bytes 4194328
  18.4 0.9 %shard_map.120.own_ref = f32[112,256]{1,0:T(8,128)S(1)} custom-call(s32[1,16]{1,0:T(1,128)S(1)} %copy-done.7, s32[1]{0:T(128)S(6)} %copy.14.count_ref, s32[1]{0:T(128)S(6)} %copy.13.band_points_ref.limit_ref, bf16[16,256,512]{2,1,0:T(8,128)(2,1)S(1)} %bitcast.3, bf16[100,16384]{1,0:T(8,128)(2,1)S(1)} %copy-done.1), custom_call_target="tpu_custom_call" | custom-call | flops 838860800 | bytes 1048576 | tf_op jit(solution)/shard_map/pallas_call | solution.py:249
  19.4 8.4 %collective-permute-done.early_ref = bf16[8,38400]{1,0:T(8,128)(2,1)S(1)} collective-permute-done((bf16[8,38400]{1,0:T(8,128)(2,1)S(1)}, bf16[8,38400]{1,0:T(8,128)(2,1)S(1)}, u32[]{:S(2)}, u32[]{:S(2)}) %collective-permute-start) | collective-permute-done | bytes 614432 | tf_op jit(solution)/shard_map/ppermute | solution.py:303
  27.9 1.9 %shard_map.121 = f32[112,256]{1,0:T(8,128)S(1)} custom-call(s32[1,16]{1,0:T(1,128)S(1)} %copy-done.7, s32[1]{0:T(128)S(6)} %copy.14.count_ref, bf16[16,256,512]{2,1,0:T(8,128)(2,1)S(1)} %bitcast.4, bf16[8,38400]{1,0:T(8,128)(2,1)S(1)} %collective-permute-done.early_ref, bf16[8,64000]{1,0:T(8,128)(2,1)} %collective-permute-done.1.late_ref, ...), custom_call_target="tpu_custom_call" | custom-call | flops 104857600 | bytes 1048576 | tf_op jit(solution)/shard_map/pallas_call | solution.py:249
  29.7 4.1 %collective-permute-start.2 = (f32[112,256]{1,0:T(8,128)S(1)}, f32[112,256]{1,0:T(8,128)S(1)}, u32[]{:S(2)}, u32[]{:S(2)}) collective-permute-start(f32[112,256]{1,0:T(8,128)S(1)} %shard_map.121), channel_id=1, source_target_pairs={{0,1},{1,0},{2,3},{3,2},{4,5},{5,4},{6,7},{7,6},{8,9},{9,8},{10,11... | collective-permute-start | bytes 344072 | tf_op jit(solution)/shard_map/ppermute | solution.py:308
  34.0 0.6 %shard_map.123 = (bf16[256,5120]{1,0:T(8,128)(2,1)S(1)}, bf16[256,5120]{1,0:T(8,128)(2,1)S(1)}) custom-call(s32[1,5120]{1,0:T(1,128)S(1)} %bitcast.5, s32[1,5120]{1,0:T(1,128)S(1)} %bitcast.8), custom_call_target="tpu_custom_call" | custom-call | flops 20971520 | bytes 1048576 | tf_op jit(solution)/shard_map/pallas_call | solution.py:249
  34.8 4.2 %collective-permute-start.4 = (bf16[112,256]{1,0:T(8,128)(2,1)S(1)}, bf16[112,256]{1,0:T(8,128)(2,1)S(1)}, u32[]{:S(2)}, u32[]{:S(2)}) collective-permute-start(bf16[112,256]{1,0:T(8,128)(2,1)S(1)} %add_convert_fusion.mid_ref), channel_id=1, source_target_pairs={{2,4},{3,5},{4,2},{5,3},{6,8},{7,9},{8,6},{9,7},{10,12},{11,13},{1... | collective-permute-start | bytes 172040 | tf_op jit(solution)/shard_map/ppermute | solution.py:374
  39.1 0.9 %shard_map.124.gathered_ref = bf16[224,5120]{1,0:T(8,128)(2,1)S(1)} custom-call(bf16[112,256]{1,0:T(8,128)(2,1)S(1)} %add_convert_fusion.mid_ref, s32[1,5120]{1,0:T(1,128)S(1)} %bitcast.6, bf16[256,5120]{1,0:T(8,128)(2,1)S(1)} %get-tuple-element.12.from_ref, bf16[256,5120]{1,0:T(8,128)(2,1)S(1)} %get-tuple-element.13.to_ref), custom_call_target="tpu_custom_call" | custom-call | flops 587202560 | bytes 1048576 | tf_op jit(solution)/shard_map/pallas_call | solution.py:249
  40.0 0.3 collective-permute-start.3
  40.4 0.3 copy-done.3
  40.7 0.6 %copy-done.4 = bf16[2,1024,512]{2,1,0:T(8,128)(2,1)S(1)} copy-done((bf16[2,1024,512]{2,1,0:T(8,128)(2,1)S(1)}, bf16[2,1024,512]{2,1,0:T(8,128)(2,1)}, u32[]{:S(2)}) %copy-start.4) | copy-done | bytes 2097176
  41.3 5.3 %shard_map.122 = (bf16[224,512]{1,0:T(8,128)(2,1)S(1)}, bf16[112,1024]{1,0:T(8,128)(2,1)S(1)}, bf16[2,512,1024]{2,1,0:T(8,128)(2,1)S(1)}, bf16[2,512,512]{2,1,0:T(8,128)(2,1)S(1)}) custom-call(bf16[100,512]{1,0:T(8,128)(2,1)S(1)} %copy-done.5, bf16[100,512]{1,0:T(8,128)(2,1)S(1)} %collective-permute-done.5.embed_other_ref, ...), custom_call_target="tpu_custom_call" | custom-call | flops 2147483648 | bytes 1048576 | tf_op jit(solution)/shard_map/pallas_call | solution.py:249
  46.7 3.6 %shard_map.125.own_ref = bf16[256,512]{1,0:T(8,128)(2,1)S(1)} custom-call(bf16[112,256]{1,0:T(8,128)(2,1)S(1)} %collective-permute-done.3.near_ref, bf16[112,256]{1,0:T(8,128)(2,1)S(1)} %collective-permute-done.4.far_ref, bf16[224,512]{1,0:T(8,128)(2,1)S(1)} %get-tuple-element.11.into_ref, s32[1,5120]{1,0:T(1,128)S(1)} %bitcast.7, ...), custom_call_target="tpu_custom_call" | custom-call | flops 4697620480 | bytes 1048576 | tf_op jit(solution)/shard_map/pallas_call | solution.py:249
  50.3 0.5 collective-permute-start.9
  50.8 1.2 %collective-permute-done.9.other_ref = bf16[256,512]{1,0:T(8,128)(2,1)S(1)} collective-permute-done((bf16[256,512]{1,0:T(8,128)(2,1)S(1)}, bf16[256,512]{1,0:T(8,128)(2,1)S(1)}, u32[]{:S(2)}, u32[]{:S(2)}) %collective-permute-start.9) | collective-permute-done | bytes 262176 | tf_op jit(solution)/shard_map/ppermute | solution.py:308
  52.0 1.9 %shard_map.126 = bf16[256,512]{1,0:T(8,128)(2,1)} custom-call(bf16[256,512]{1,0:T(8,128)(2,1)S(1)} %shard_map.125.own_ref, bf16[256,512]{1,0:T(8,128)(2,1)S(1)} %collective-permute-done.9.other_ref, bf16[112,256]{1,0:T(8,128)(2,1)S(1)} %add_convert_fusion.mid_ref, bf16[112,1024]{1,0:T(8,128)(2,1)S(1)} %get-tuple-element.14.direct_ref, ...), custom_call_target="tpu_custom_call" | custom-call | flops 805306368 | bytes 1048576 | tf_op jit(solution)/shard_map/pallas_call | solution.py:249
  (24 shorter events, 0.4 us)
Async XLA Ops:
  0.0 40.3 %collective-permute-start.6 = (bf16[2,1024,512]{2,1,0:T(8,128)(2,1)}, bf16[2,1024,512]{2,1,0:T(8,128)(2,1)S(1)}, u32[]{:S(2)}, u32[]{:S(2)}) collective-permute-start(bf16[2,1024,512]{2,1,0:T(8,128)(2,1)} %node_own_ref.1), channel_id=1, source_target_pairs={{0,1},{1,0},{2,3},{3,2},{4,5},{5,4},{6,7},{7,6},{8,9},{9,8},{10,11... | collective-permute-start | bytes 6291464 | tf_op jit(solution)/shard_map/ppermute | solution.py:308
  1.3 2.0 %copy-start = (bf16[100,16384]{1,0:T(8,128)(2,1)S(1)}, bf16[100,16384]{1,0:T(8,128)(2,1)}, u32[]{:S(2)}) copy-start(bf16[100,16384]{1,0:T(8,128)(2,1)} %points_ref.5) | copy-start | bytes 9830404
  5.0 9.2 %copy-start.7 = (s32[1,16]{1,0:T(1,128)S(1)}, s32[1,16]{1,0:T(1,128)}, u32[]{:S(2)}) copy-start(s32[1,16]{1,0:T(1,128)} %ids_ref.3) | copy-start | bytes 196
  5.0 22.8 %collective-permute-start.1 = (bf16[8,64000]{1,0:T(8,128)(2,1)}, bf16[8,64000]{1,0:T(8,128)(2,1)}, u32[]{:S(2)}, u32[]{:S(2)}) collective-permute-start(bf16[8,64000]{1,0:T(8,128)(2,1)} %shard_map.119), channel_id=1, source_target_pairs={{0,2},{2,4},{4,6},{6,8},{8,10},{10,12},{12,14},{14,16},{16,18},{18... | collective-permute-start | bytes 3072008 | tf_op jit(solution)/shard_map/ppermute | solution.py:303
  9.6 30.7 %collective-permute-start.7 = (bf16[512,1024]{1,0:T(8,128)(2,1)}, bf16[512,1024]{1,0:T(8,128)(2,1)}, u32[]{:S(2)}, u32[]{:S(2)}) collective-permute-start(bf16[512,1024]{1,0:T(8,128)(2,1)} %out_own_ref.1), channel_id=1, source_target_pairs={{0,1},{1,0},{2,3},{3,2},{4,5},{5,4},{6,7},{7,6},{8,9},{9,8},{10,11... | collective-permute-start | bytes 3145736 | tf_op jit(solution)/shard_map/ppermute | solution.py:308
  9.6 30.8 %collective-permute-start.8 = (bf16[512,1024]{1,0:T(8,128)(2,1)}, bf16[512,1024]{1,0:T(8,128)(2,1)}, u32[]{:S(2)}, u32[]{:S(2)}) collective-permute-start(bf16[512,1024]{1,0:T(8,128)(2,1)} %last_own_hbm.1), channel_id=1, source_target_pairs={{0,1},{1,0},{2,3},{3,2},{4,5},{5,4},{6,7},{7,6},{8,9},{9,8},{10,11... | collective-permute-start | bytes 3145736 | tf_op jit(solution)/shard_map/ppermute | solution.py:308
  11.3 16.5 %collective-permute-start = (bf16[8,38400]{1,0:T(8,128)(2,1)S(1)}, bf16[8,38400]{1,0:T(8,128)(2,1)S(1)}, u32[]{:S(2)}, u32[]{:S(2)}) collective-permute-start(bf16[8,38400]{1,0:T(8,128)(2,1)S(1)} %shard_map.118), channel_id=1, source_target_pairs={{0,2},{2,4},{4,6},{6,8},{8,10},{10,12},{12,14},{14,16},{16,18},{18... | collective-permute-start | bytes 1843208 | tf_op jit(solution)/shard_map/ppermute | solution.py:303
  14.3 2.0 %copy-start.1 = (bf16[100,16384]{1,0:T(8,128)(2,1)S(1)}, bf16[100,16384]{1,0:T(8,128)(2,1)}, u32[]{:S(2)}) copy-start(bf16[100,16384]{1,0:T(8,128)(2,1)} %points_ref.5) | copy-start | bytes 9830404
  16.2 2.2 %copy-start.2 = (bf16[1,16,256,512]{3,2,1,0:T(8,128)(2,1)S(1)}, bf16[1,16,256,512]{3,2,1,0:T(8,128)(2,1)}, u32[]{:S(2)}) copy-start(bf16[1,16,256,512]{3,2,1,0:T(8,128)(2,1)} %param.16) | copy-start | bytes 12582916
  19.4 14.5 %copy-start.5 = (bf16[100,512]{1,0:T(8,128)(2,1)S(1)}, bf16[100,512]{1,0:T(8,128)(2,1)}, u32[]{:S(2)}) copy-start(bf16[100,512]{1,0:T(8,128)(2,1)} %embed_ref.3) | copy-start | bytes 307204
  19.4 14.6 %copy-start.6 = (s32[5120]{0:T(1024)S(1)}, s32[5120]{0:T(1024)}, u32[]{:S(2)}) copy-start(s32[5120]{0:T(1024)} %param.18) | copy-start | bytes 61444
  19.4 14.6 %copy-start.8 = (s32[5120]{0:T(1024)S(1)}, s32[5120]{0:T(1024)}, u32[]{:S(2)}) copy-start(s32[5120]{0:T(1024)} %param.19) | copy-start | bytes 61444
  29.7 5.1 %collective-permute-start.2 = (f32[112,256]{1,0:T(8,128)S(1)}, f32[112,256]{1,0:T(8,128)S(1)}, u32[]{:S(2)}, u32[]{:S(2)}) collective-permute-start(f32[112,256]{1,0:T(8,128)S(1)} %shard_map.121), channel_id=1, source_target_pairs={{0,1},{1,0},{2,3},{3,2},{4,5},{5,4},{6,7},{7,6},{8,9},{9,8},{10,11... | collective-permute-start | bytes 344072 | tf_op jit(solution)/shard_map/ppermute | solution.py:308
  33.8 6.2 %collective-permute-start.5 = (bf16[100,512]{1,0:T(8,128)(2,1)S(1)}, bf16[100,512]{1,0:T(8,128)(2,1)S(1)}, u32[]{:S(2)}, u32[]{:S(2)}) collective-permute-start(bf16[100,512]{1,0:T(8,128)(2,1)S(1)} %copy-done.5), channel_id=1, source_target_pairs={{0,1},{1,0},{2,3},{3,2},{4,5},{5,4},{6,7},{7,6},{8,9},{9,8},{10,11... | collective-permute-start | bytes 307208 | tf_op jit(solution)/shard_map/ppermute | solution.py:308
  34.8 11.8 %collective-permute-start.4 = (bf16[112,256]{1,0:T(8,128)(2,1)S(1)}, bf16[112,256]{1,0:T(8,128)(2,1)S(1)}, u32[]{:S(2)}, u32[]{:S(2)}) collective-permute-start(bf16[112,256]{1,0:T(8,128)(2,1)S(1)} %add_convert_fusion.mid_ref), channel_id=1, source_target_pairs={{2,4},{3,5},{4,2},{5,3},{6,8},{7,9},{8,6},{9,7},{10,12},{11,13},{1... | collective-permute-start | bytes 172040 | tf_op jit(solution)/shard_map/ppermute | solution.py:374
  39.1 1.6 %copy-start.3 = (bf16[2,1024,512]{2,1,0:T(8,128)(2,1)S(1)}, bf16[2,1024,512]{2,1,0:T(8,128)(2,1)}, u32[]{:S(2)}) copy-start(bf16[2,1024,512]{2,1,0:T(8,128)(2,1)} %edge_in_ref.1) | copy-start | bytes 6291460
  39.1 2.2 %copy-start.4 = (bf16[2,1024,512]{2,1,0:T(8,128)(2,1)S(1)}, bf16[2,1024,512]{2,1,0:T(8,128)(2,1)}, u32[]{:S(2)}) copy-start(bf16[2,1024,512]{2,1,0:T(8,128)(2,1)} %node_own_ref.1) | copy-start | bytes 6291460
  40.0 6.6 %collective-permute-start.3 = (bf16[112,256]{1,0:T(8,128)(2,1)S(1)}, bf16[112,256]{1,0:T(8,128)(2,1)S(1)}, u32[]{:S(2)}, u32[]{:S(2)}) collective-permute-start(bf16[112,256]{1,0:T(8,128)(2,1)S(1)} %add_convert_fusion.mid_ref), channel_id=1, source_target_pairs={{0,2},{1,3},{2,0},{3,1},{4,6},{5,7},{6,4},{7,5},{8,10},{9,11},{10,... | collective-permute-start | bytes 172040 | tf_op jit(solution)/shard_map/ppermute | solution.py:374
  50.3 1.7 %collective-permute-start.9 = (bf16[256,512]{1,0:T(8,128)(2,1)S(1)}, bf16[256,512]{1,0:T(8,128)(2,1)S(1)}, u32[]{:S(2)}, u32[]{:S(2)}) collective-permute-start(bf16[256,512]{1,0:T(8,128)(2,1)S(1)} %shard_map.125.own_ref), channel_id=1, source_target_pairs={{0,1},{1,0},{2,3},{3,2},{4,5},{5,4},{6,7},{7,6},{8,9},{9,8},{10,11... | collective-permute-start | bytes 786440 | tf_op jit(solution)/shard_map/ppermute | solution.py:308
